TPU v7x, 16 devices: a whole 2x2x2 slice. The times are simulated.
16 devices in a mesh: data: 16 (over z, y, x, core).
Axes of the slice: x: 2, y: 2, z: 2, core: 2. Of those that a mesh axis runs over, the one named last changes fastest.
Arguments:
- tokens: bfloat16 [16384, 1536], P('data')
- upstream: bfloat16 [16384, 1536], P('data')
- norm_gain: bfloat16 [2, 1536], replicated
- w_up: bfloat16 [2, 1536, 6144], replicated
- bias_up: bfloat16 [2, 6144], replicated
- w_down: bfloat16 [2, 6144, 1536], replicated
- bias_down: bfloat16 [2, 1536], replicated
Outputs:
- output 1: float32 [2, 1536], replicated
- output 2: float32 [2, 1536, 6144], replicated
- output 3: float32 [2, 6144], replicated
- output 4: float32 [2, 6144, 1536], replicated
- output 5: float32 [2, 1536], replicated
All inputs are finite; a program needn't handle non-finite values.
Results may differ from a plain program's by a relative error of at most 0.0070572.
Values are sent between devices in bfloat16 or wider.
A program may use at most 1 GiB of HBM per device.

v0:
```python
import jax
import jax.numpy as jnp
from jax import lax
from jax.sharding import PartitionSpec as P

EPSILON = 1e-6
TOKEN_DIMS = (((0,), (0,)), ((), ()))
FEATURE_DIMS = (((1,), (1,)), ((), ()))


def gelu_tanh(values):
    return jax.nn.gelu(values, approximate=True)


def inverse_rms(hid_f):
    return lax.rsqrt(jnp.mean(hid_f * hid_f, axis=-1, keepdims=True) + EPSILON)


def forward_stack(hidden, norm_gain, w_up, bias_up, w_down, bias_down):
    saved_acts = []
    for layer_idx in range(norm_gain.shape[0]):
        hid_f = hidden.astype(jnp.float32)
        hid_scale = inverse_rms(hid_f)
        hid_hat = hid_f * hid_scale
        normed = (hid_hat * norm_gain[layer_idx].astype(jnp.float32)).astype(jnp.bfloat16)
        pre_act = (jnp.dot(normed, w_up[layer_idx], preferred_element_type=jnp.float32) + bias_up[layer_idx].astype(jnp.float32)).astype(jnp.bfloat16)
        activated = gelu_tanh(pre_act.astype(jnp.float32)).astype(jnp.bfloat16)
        branch = jnp.dot(activated, w_down[layer_idx], preferred_element_type=jnp.float32)
        hidden = (hid_f + branch + bias_down[layer_idx].astype(jnp.float32)).astype(jnp.bfloat16)
        saved_acts.append((hid_scale, hid_hat, normed, pre_act, activated))
    return hidden, saved_acts


def top_gradient(top_hidden, upstream):
    top_f = top_hidden.astype(jnp.float32)
    top_scale = inverse_rms(top_f)
    top_hat = top_f * top_scale
    up_f = upstream.astype(jnp.float32)
    return top_scale * (up_f - top_hat * jnp.mean(up_f * top_hat, axis=-1, keepdims=True))


def layer_backward(grad_h, saved_layer, gain_row, up_mat, down_mat, need_input):
    hid_scale, hid_hat, normed, pre_act, activated = saved_layer
    grad_b = grad_h.astype(jnp.bfloat16)
    grad_down = lax.dot_general(activated, grad_b, TOKEN_DIMS, preferred_element_type=jnp.float32)
    grad_down_bias = jnp.sum(grad_h, axis=0)
    grad_act = lax.dot_general(grad_b, down_mat, FEATURE_DIMS, preferred_element_type=jnp.float32)
    gelu_back = jax.vjp(gelu_tanh, pre_act.astype(jnp.float32))[1]
    grad_pre = gelu_back(grad_act)[0]
    grad_pre_b = grad_pre.astype(jnp.bfloat16)
    grad_up = lax.dot_general(normed, grad_pre_b, TOKEN_DIMS, preferred_element_type=jnp.float32)
    grad_up_bias = jnp.sum(grad_pre, axis=0)
    grad_normed = lax.dot_general(grad_pre_b, up_mat, FEATURE_DIMS, preferred_element_type=jnp.float32)
    grad_gain = jnp.sum(grad_normed * hid_hat, axis=0)
    layer_grads = (grad_gain, grad_up, grad_up_bias, grad_down, grad_down_bias)
    if not need_input:
        return layer_grads, None
    grad_hat = grad_normed * gain_row.astype(jnp.float32)
    grad_new = grad_h + hid_scale * (grad_hat - hid_hat * jnp.mean(grad_hat * hid_hat, axis=-1, keepdims=True))
    return layer_grads, grad_new


def solution(mesh):
    data_axis = mesh.axis_names[0]

    def device_grads(tokens, upstream, norm_gain, w_up, bias_up, w_down, bias_down):
        top_hidden, saved_acts = forward_stack(tokens, norm_gain, w_up, bias_up, w_down, bias_down)
        grad_h = top_gradient(top_hidden, upstream)
        num_layers = norm_gain.shape[0]
        reduced = [None] * num_layers
        for layer_idx in reversed(range(num_layers)):
            local_grads, grad_h = layer_backward(grad_h, saved_acts[layer_idx], norm_gain[layer_idx], w_up[layer_idx], w_down[layer_idx], layer_idx > 0)
            reduced[layer_idx] = lax.psum(local_grads, data_axis)
        return tuple(jnp.stack([reduced[layer_idx][which_grad] for layer_idx in range(num_layers)]) for which_grad in range(5))

    row_spec = P(data_axis, None)
    full_spec = P()
    return jax.shard_map(
        device_grads,
        mesh=mesh,
        in_specs=(row_spec, row_spec, full_spec, full_spec, full_spec, full_spec, full_spec),
        out_specs=(full_spec, full_spec, full_spec, full_spec, full_spec),
        check_vma=False,
    )
```

profile of v0, /device:TPU:0, one launch (start us, length us, event | category | flops | bytes accessed | tf_op | source)
XLA Modules:
  0.0 1758.0 jit_solution(14425172135788451911)
XLA Ops:
  8.0 0.9 slice_convert_fusion
  8.9 0.8 convert_reduce_fusion.1
  9.7 2.6 fusion.62
  12.3 26.0 %add_convert_fusion.1 = bf16[1024,6144]{1,0:T(8,128)(2,1)} fusion(f32[6144]{0:T(1024)S(1)} %bitcast.65, bf16[2,1536,6144]{2,1,0:T(8,128)(2,1)} %param.10, bf16[1024,1536]{1,0:T(8,128)(2,1)} %param.7, f32[1536]{0:T(1024)S(1)} %get-tuple-element.10, f32[1024]{0:T(1024)S(1)} %add_rsqrt_fusion.2), kind=kOutput, calls=%fused_computation.35 | convolution fusion | flops 19346227200 | bytes 34637824 | tf_op jit(solution)/shard_map/dot_general | solution.py:26
  38.3 39.8 %fusion.71 = (f32[1024]{0:T(1024)S(1)}, bf16[1024,1536]{1,0:T(8,128)(2,1)}) fusion(f32[1536]{0:T(1024)S(1)} %get-tuple-element.8, bf16[2,6144,1536]{2,1,0:T(8,128)(2,1)} %param.12, bf16[1024,6144]{1,0:T(8,128)(2,1)} %add_convert_fusion.1, bf16[1024,1536]{1,0:T(8,128)(2,1)S(1)} %copy-done.3), kind=kOutput, calls=%fused_computation.91 | convolution fusion | flops 19401277440 | bytes 37758976 | tf_op jit(solution)/shard_map/dot_general | solution.py:28
  78.1 25.9 %add_convert_fusion = bf16[1024,6144]{1,0:T(8,128)(2,1)} fusion(f32[6144]{0:T(1024)S(1)} %bitcast.64, bf16[2,1536,6144]{2,1,0:T(8,128)(2,1)} %param.10, bf16[1024,1536]{1,0:T(8,128)(2,1)} %get-tuple-element.26, f32[1536]{0:T(1024)S(1)} %get-tuple-element.9, f32[1024]{0:T(1024)S(1)} %add_rsqrt_fusion.1), kind=kOutput, calls=%fused_computation.34 | convolution fusion | flops 19346227200 | bytes 34637824 | tf_op jit(solution)/shard_map/dot_general | solution.py:26
  104.0 34.9 %fusion.59 = (f32[1024]{0:T(1024)S(1)}, bf16[1024,1536]{1,0:T(8,128)(2,1)}) fusion(f32[1536]{0:T(1024)S(1)} %get-tuple-element.7, bf16[2,6144,1536]{2,1,0:T(8,128)(2,1)} %param.12, bf16[1024,6144]{1,0:T(8,128)(2,1)} %add_convert_fusion, bf16[1024,1536]{1,0:T(8,128)(2,1)} %get-tuple-element.26), kind=kOutput, calls=%fused_computation.79 | convolution fusion | flops 19401277440 | bytes 37758976 | tf_op jit(solution)/shard_map/dot_general | solution.py:28
  138.9 3.1 fusion.60
  142.0 41.4 %fusion.102 = (f32[6144]{0:T(1024)}, bf16[1024,6144]{1,0:T(8,128)(2,1)}) fusion(bf16[1024,6144]{1,0:T(8,128)(2,1)} %add_convert_fusion, bf16[2,6144,1536]{2,1,0:T(8,128)(2,1)} %param.12, bf16[1024,1536]{1,0:T(8,128)(2,1)} %get-tuple-element.28, bf16[1024,1536]{1,0:T(8,128)(2,1)S(1)} %copy-done, f32[1024]{0:T(1024)S(1)} %broadcast_multiply_fusion.1, ...), kind=kOutput, calls=%fused_computation.117 | convolution fusion | flops 19476768768 | bytes 50364416 | tf_op jit(solution)/shard_map/dot_general | solution.py:47
  183.4 29.4 %fusion.66 = (f32[1024]{0:T(1024)S(1)}, f32[1536]{0:T(1024)S(1)}, f32[1024,1536]{1,0:T(8,128)}) fusion(bf16[1024,1536]{1,0:T(8,128)(2,1)} %get-tuple-element.26, f32[1536]{0:T(1024)S(1)} %copy-done.8, f32[1024]{0:T(1024)S(1)} %copy-done.10, bf16[2,1536,6144]{2,1,0:T(8,128)(2,1)} %param.10, bf16[1024,6144]{1,0:T(8,128)(2,1)} %get-tuple-element.31), kind=kOutput, calls=%fused_computation.86 | convolution fusion | flops 19338360832 | bytes 40914944 | tf_op jit(solution)/shard_map/dot_general | solution.py:53
  213.4 6.6 fusion.100
  220.0 41.0 %fusion.103 = (f32[6144]{0:T(1024)}, bf16[1024,6144]{1,0:T(8,128)(2,1)}) fusion(bf16[1024,6144]{1,0:T(8,128)(2,1)} %add_convert_fusion.1, bf16[2,6144,1536]{2,1,0:T(8,128)(2,1)} %param.12, bf16[1024,1536]{1,0:T(8,128)(2,1)S(1)} %get-tuple-element.21), kind=kOutput, calls=%fused_computation.118 | convolution fusion | flops 19465758720 | bytes 47210496 | tf_op jit(solution)/shard_map/dot_general | solution.py:47
  261.0 26.7 %fusion.58 = f32[1536]{0:T(1024)S(1)} fusion(bf16[1024,1536]{1,0:T(8,128)(2,1)S(1)} %copy-done.4, f32[1024]{0:T(1024)S(1)} %copy-done.14, bf16[2,1536,6144]{2,1,0:T(8,128)(2,1)} %param.10, bf16[1024,6144]{1,0:T(8,128)(2,1)} %get-tuple-element.33), kind=kOutput, calls=%fused_computation.78 | convolution fusion | flops 19333642240 | bytes 34613248 | tf_op jit(solution)/shard_map/dot_general | solution.py:53
  289.6 29.1 %convolution_bitcast_fusion = f32[1,1536,6144]{2,1,0:T(8,128)} fusion(bf16[1024,6144]{1,0:T(8,128)(2,1)} %get-tuple-element.31, bf16[1024,1536]{1,0:T(8,128)(2,1)} %get-tuple-element.26, f32[1536]{0:T(1024)S(1)} %copy-done.8, f32[1024]{0:T(1024)S(1)} %copy-done.10), kind=kOutput, calls=%fused_computation.14 | convolution fusion | flops 19333644288 | bytes 53487616 | tf_op jit(solution)/shard_map/dot_general | solution.py:51
  318.7 35.8 %convolution_bitcast_fusion.2 = f32[1,6144,1536]{2,1,0:T(8,128)} fusion(bf16[1024,6144]{1,0:T(8,128)(2,1)} %add_convert_fusion, bf16[1024,1536]{1,0:T(8,128)(2,1)S(1)} %copy-done.2, bf16[1024,1536]{1,0:T(8,128)(2,1)S(1)} %copy-done, f32[1024]{0:T(1024)S(1)} %broadcast_multiply_fusion.1, f32[1024]{0:T(1024)S(1)} %add_rsqrt_fusion), kind=kOutput, calls=%fused_computation.16 | convolution fusion | flops 19401277440 | bytes 56631296 | tf_op jit(solution)/shard_map/dot_general | solution.py:45
  354.5 29.2 %convolution_bitcast_fusion.1 = f32[1,1536,6144]{2,1,0:T(8,128)} fusion(bf16[1024,6144]{1,0:T(8,128)(2,1)} %get-tuple-element.33, bf16[1024,1536]{1,0:T(8,128)(2,1)} %param.7, f32[1536]{0:T(1024)S(1)} %copy-done.12, f32[1024]{0:T(1024)S(1)} %copy-done.14), kind=kOutput, calls=%fused_computation.15 | convolution fusion | flops 19333644288 | bytes 53487616 | tf_op jit(solution)/shard_map/dot_general | solution.py:51
  383.7 1.8 copy-done.6
  385.6 32.0 %convolution_bitcast_fusion.3 = f32[1,6144,1536]{2,1,0:T(8,128)} fusion(bf16[1024,1536]{1,0:T(8,128)(2,1)S(1)} %copy-done.6, bf16[1024,6144]{1,0:T(8,128)(2,1)} %add_convert_fusion.1), kind=kOutput, calls=%fused_computation.17 | convolution fusion | flops 19390267392 | bytes 53477376 | tf_op jit(solution)/shard_map/dot_general | solution.py:45
  417.6 1.4 pad_maximum_fusion.3
  419.0 1.4 pad_maximum_fusion.2
  420.4 926.4 %all-reduce.10.cloned.1.call-done = (f32[1,1536,6144]{2,1,0:T(8,128)}, f32[1,1536,6144]{2,1,0:T(8,128)}, f32[1,6144,1536]{2,1,0:T(8,128)}) async-done(((f32[1,1536,6144]{2,1,0:T(8,128)}, f32[1,1536,6144]{2,1,0:T(8,128)}, f32[1,6144,1536]{2,1,0:T(8,128)}), (f32[1,1536,6144]{2,1,0:T(8,128)}, f32[1,1536,6144]{2,1,0:T(8,128)}, f32[1,6144,1536]{2,1,0:T(8,128)})) %all-reduce.10.cloned.1.call-update) | async-done | bytes 113246224 | tf_op jit(solution)/shard_map/psum | solution.py:73
  1346.8 48.9 %pad_maximum_fusion = f32[2,1536,6144]{2,1,0:T(8,128)} fusion(f32[1,1536,6144]{2,1,0:T(8,128)} %get-tuple-element.17, f32[1,1536,6144]{2,1,0:T(8,128)} %get-tuple-element.18), kind=kLoop, calls=%fused_computation | loop fusion | flops 18874368 | bytes 150994944 | tf_op jit(solution)/shard_map/stack | solution.py:74
  1395.7 306.4 %all-reduce.6.cloned.1.call-done = f32[1,6144,1536]{2,1,0:T(8,128)} async-done(((f32[1,6144,1536]{2,1,0:T(8,128)}), f32[1,6144,1536]{2,1,0:T(8,128)}) %all-reduce.6.cloned.1.call-update) | async-done | bytes 37748752 | tf_op jit(solution)/shard_map/psum | solution.py:73
  1702.0 49.3 %pad_maximum_fusion.1 = f32[2,6144,1536]{2,1,0:T(8,128)} fusion(f32[1,6144,1536]{2,1,0:T(8,128)} %get-tuple-element.19, f32[1,6144,1536]{2,1,0:T(8,128)} %all-reduce.6.cloned.1.call-done), kind=kLoop, calls=%fused_computation.1 | loop fusion | flops 18874368 | bytes 150994944 | tf_op jit(solution)/shard_map/stack | solution.py:74
  (46 shorter events, 3.5 us)
Async XLA Ops:
  7.2 410.5 %all-reduce.8.cloned.1.call-start = ((), (), s32[]{:S(2)}) async-start(), calls=%async_computation.1 | async-start | bytes 147456 | tf_op jit(solution)/shard_map/psum | solution.py:73
  9.7 28.6 %copy-start.11 = (f32[1536]{0:T(1024)}, f32[1536]{0:T(1024)S(1)}, u32[]{:S(2)}) copy-start(f32[1536]{0:T(1024)S(1)} %get-tuple-element.10) | copy-start | bytes 18436
  9.7 68.4 %copy-start.7 = (f32[1536]{0:T(1024)}, f32[1536]{0:T(1024)S(1)}, u32[]{:S(2)}) copy-start(f32[1536]{0:T(1024)S(1)} %get-tuple-element.9) | copy-start | bytes 18436
  12.3 26.0 %copy-start.13 = (f32[1024]{0:T(1024)}, f32[1024]{0:T(1024)S(1)}, u32[]{:S(2)}) copy-start(f32[1024]{0:T(1024)S(1)} %add_rsqrt_fusion.2) | copy-start | bytes 12292
  12.3 26.0 %copy-start.3 = (bf16[1024,1536]{1,0:T(8,128)(2,1)S(1)}, bf16[1024,1536]{1,0:T(8,128)(2,1)}, u32[]{:S(2)}) copy-start(bf16[1024,1536]{1,0:T(8,128)(2,1)} %param.7) | copy-start | bytes 9437188
  78.1 25.9 %copy-start.9 = (f32[1024]{0:T(1024)}, f32[1024]{0:T(1024)S(1)}, u32[]{:S(2)}) copy-start(f32[1024]{0:T(1024)S(1)} %add_rsqrt_fusion.1) | copy-start | bytes 12292
  104.0 34.9 %copy-start = (bf16[1024,1536]{1,0:T(8,128)(2,1)S(1)}, bf16[1024,1536]{1,0:T(8,128)(2,1)}, u32[]{:S(2)}) copy-start(bf16[1024,1536]{1,0:T(8,128)(2,1)} %param.8) | copy-start | bytes 9437188
  142.0 41.4 %copy-start.8 = (f32[1536]{0:T(1024)S(1)}, f32[1536]{0:T(1024)}, u32[]{:S(2)}) copy-start(f32[1536]{0:T(1024)} %copy-done.7) | copy-start | bytes 18436
  142.0 41.4 %copy-start.10 = (f32[1024]{0:T(1024)S(1)}, f32[1024]{0:T(1024)}, u32[]{:S(2)}) copy-start(f32[1024]{0:T(1024)} %copy-done.9) | copy-start | bytes 12292
  183.4 30.0 %copy-start.1 = (bf16[1024,1536]{1,0:T(8,128)(2,1)S(1)}, bf16[1024,1536]{1,0:T(8,128)(2,1)}, u32[]{:S(2)}) copy-start(bf16[1024,1536]{1,0:T(8,128)(2,1)} %get-tuple-element.28) | copy-start | bytes 9437188
  220.0 41.0 %copy-start.5 = (bf16[1024,1536]{1,0:T(8,128)(2,1)}, bf16[1024,1536]{1,0:T(8,128)(2,1)S(1)}, u32[]{:S(2)}) copy-start(bf16[1024,1536]{1,0:T(8,128)(2,1)S(1)} %get-tuple-element.21) | copy-start | bytes 9437188
  220.0 41.0 %copy-start.4 = (bf16[1024,1536]{1,0:T(8,128)(2,1)S(1)}, bf16[1024,1536]{1,0:T(8,128)(2,1)}, u32[]{:S(2)}) copy-start(bf16[1024,1536]{1,0:T(8,128)(2,1)} %param.7) | copy-start | bytes 9437188
  220.0 41.0 %copy-start.14 = (f32[1024]{0:T(1024)S(1)}, f32[1024]{0:T(1024)}, u32[]{:S(2)}) copy-start(f32[1024]{0:T(1024)} %copy-done.13) | copy-start | bytes 12292
  289.6 1057.2 %all-reduce.10.cloned.1.call-start = ((), (), s32[]{:S(2)}) async-start(), calls=%async_computation.2 | async-start | bytes 226492416 | tf_op jit(solution)/shard_map/psum | solution.py:73
  289.6 29.1 %copy-start.2 = (bf16[1024,1536]{1,0:T(8,128)(2,1)S(1)}, bf16[1024,1536]{1,0:T(8,128)(2,1)}, u32[]{:S(2)}) copy-start(bf16[1024,1536]{1,0:T(8,128)(2,1)} %get-tuple-element.28) | copy-start | bytes 9437188
  318.7 35.8 %copy-start.12 = (f32[1536]{0:T(1024)S(1)}, f32[1536]{0:T(1024)}, u32[]{:S(2)}) copy-start(f32[1536]{0:T(1024)} %copy-done.11) | copy-start | bytes 18436
  383.7 1.9 copy-start.6
  383.7 1318.4 %all-reduce.6.cloned.1.call-start = ((), (), s32[]{:S(2)}) async-start(), calls=%async_computation | async-start | bytes 75497472 | tf_op jit(solution)/shard_map/psum | solution.py:73
Sparse Core Ops, SparseCore 0:
  289.7 70.3 all-reduce.7
  383.8 962.9 all-reduce.9
  1352.5 349.5 all-reduce.5
where the time goes:
time: 1760 us
  waiting for transfers between devices  1230 us (70%)
  matrix products  391 us (22%)
  other arithmetic  116 us (7%)
    psum x3, waiting for transfers between devices, device_grads(): reduced[layer_idx] = lax.psum(local_grads, data_axis)  1230 us
    another operation x4, other arithmetic, device_grads(): jnp.stack([reduced[layer_idx][which_grad] for layer_idx in range(num_laye...  101 us
    dot_general x2, matrix products, layer_backward(): lax.dot_general(grad_b, down_mat, FEATURE_DIMS, preferred_element_type=jn...  82.3 us
    dot_general x2, matrix products, forward_stack(): jnp.dot(activated, w_down[layer_idx], preferred_element_type=jnp.float32)  74.6 us
    dot_general x2, matrix products, layer_backward(): lax.dot_general(activated, grad_b, TOKEN_DIMS, preferred_element_type=jnp...  67.8 us
    dot_general x2, matrix products, layer_backward(): lax.dot_general(normed, grad_pre_b, TOKEN_DIMS, preferred_element_type=jn...  58.2 us
    dot_general x2, matrix products, layer_backward(): lax.dot_general(grad_pre_b, up_mat, FEATURE_DIMS, preferred_element_type=...  56.2 us
    dot_general x2, matrix products, forward_stack(): jnp.dot(normed, w_up[layer_idx], preferred_element_type=jnp.float32)  51.9 us
  transfers between devices with their start and end apart: 3, of which 2 were waited for; matrix products, arithmetic and copies ran while one was open for 10% of the time, Pallas kernels for 0%

commit v1 on v0

--- a/solution.py
+++ b/solution.py
@@ -6,6 +6,9 @@
 EPSILON = 1e-6
 TOKEN_DIMS = (((0,), (0,)), ((), ()))
 FEATURE_DIMS = (((1,), (1,)), ((), ()))
+COLORS = 3
+Z_BIT, Y_BIT, X_BIT, CORE_BIT = range(4)
+COLOR_DIMS = ((X_BIT, Y_BIT, Z_BIT), (Y_BIT, Z_BIT, X_BIT), (Z_BIT, X_BIT, Y_BIT))
 
 
 def gelu_tanh(values):
@@ -39,41 +42,96 @@
     return top_scale * (up_f - top_hat * jnp.mean(up_f * top_hat, axis=-1, keepdims=True))
 
 
-def layer_backward(grad_h, saved_layer, gain_row, up_mat, down_mat, need_input):
+def flip_pairs(bit):
+    mask = 8 >> bit
+    return [(dev, dev ^ mask) for dev in range(16)]
+
+
+def pick(array, starts, sizes):
+    return lax.dynamic_slice(array, starts, sizes)
+
+
+def reduce_matrix(local, bits, axis):
+    rows, cols = local.shape
+    sub = rows // (16 * COLORS)
+    view = local.reshape(2, 2, 2, 2, COLORS, sub, cols)
+    zero = jnp.zeros((), jnp.int32)
+
+    starts = [zero] * 7
+    sizes = [2, 2, 2, 1, COLORS, sub, cols]
+    starts[CORE_BIT] = 1 - bits[CORE_BIT]
+    sent = pick(view, starts, sizes).astype(jnp.bfloat16)
+    first = lax.ppermute(sent, axis, flip_pairs(CORE_BIT))
+
+    shards = []
+    for color in range(COLORS):
+        received = [(first, CORE_BIT)]
+
+        def total(starts, sizes, received=received, color=color):
+            acc = pick(view, starts + [jnp.int32(color), zero, zero], sizes + [1, sub, cols])
+            for part, _ in received:
+                part_starts = [zero if part.shape[b] == 1 else starts[b] for b in range(4)]
+                color_start = jnp.int32(color) if part.shape[4] > 1 else zero
+                acc = acc + pick(part, part_starts + [color_start, zero, zero], sizes + [1, sub, cols]).astype(jnp.float32)
+            return acc
+
+        starts = [zero] * 4
+        sizes = [2, 2, 2, 1]
+        starts[CORE_BIT] = bits[CORE_BIT]
+        for bit in COLOR_DIMS[color]:
+            sizes[bit] = 1
+            starts[bit] = 1 - bits[bit]
+            sent = total(list(starts), list(sizes)).astype(jnp.bfloat16)
+            received.append((lax.ppermute(sent, axis, flip_pairs(bit)), bit))
+            starts[bit] = bits[bit]
+        shards.append(total(list(starts), list(sizes)).astype(jnp.bfloat16).reshape(sub, cols))
+    shard = jnp.concatenate(shards, axis=0)
+    return lax.all_gather(shard, axis, tiled=True)
+
+
+def layer_backward(grad_h, saved_layer, gain_row, up_mat, down_mat, need_input, reduce):
     hid_scale, hid_hat, normed, pre_act, activated = saved_layer
     grad_b = grad_h.astype(jnp.bfloat16)
-    grad_down = lax.dot_general(activated, grad_b, TOKEN_DIMS, preferred_element_type=jnp.float32)
+    grad_down = reduce(lax.dot_general(activated, grad_b, TOKEN_DIMS, preferred_element_type=jnp.float32))
     grad_down_bias = jnp.sum(grad_h, axis=0)
     grad_act = lax.dot_general(grad_b, down_mat, FEATURE_DIMS, preferred_element_type=jnp.float32)
     gelu_back = jax.vjp(gelu_tanh, pre_act.astype(jnp.float32))[1]
     grad_pre = gelu_back(grad_act)[0]
     grad_pre_b = grad_pre.astype(jnp.bfloat16)
-    grad_up = lax.dot_general(normed, grad_pre_b, TOKEN_DIMS, preferred_element_type=jnp.float32)
+    grad_up = reduce(lax.dot_general(normed, grad_pre_b, TOKEN_DIMS, preferred_element_type=jnp.float32))
     grad_up_bias = jnp.sum(grad_pre, axis=0)
     grad_normed = lax.dot_general(grad_pre_b, up_mat, FEATURE_DIMS, preferred_element_type=jnp.float32)
     grad_gain = jnp.sum(grad_normed * hid_hat, axis=0)
-    layer_grads = (grad_gain, grad_up, grad_up_bias, grad_down, grad_down_bias)
+    small = jnp.concatenate([grad_gain, grad_up_bias, grad_down_bias])
     if not need_input:
-        return layer_grads, None
+        return (small, grad_up, grad_down), None
     grad_hat = grad_normed * gain_row.astype(jnp.float32)
     grad_new = grad_h + hid_scale * (grad_hat - hid_hat * jnp.mean(grad_hat * hid_hat, axis=-1, keepdims=True))
-    return layer_grads, grad_new
+    return (small, grad_up, grad_down), grad_new
 
 
 def solution(mesh):
-    data_axis = mesh.axis_names[0]
+    axis = mesh.axis_names[0]
 
     def device_grads(tokens, upstream, norm_gain, w_up, bias_up, w_down, bias_down):
+        me = lax.axis_index(axis)
+        bits = [(me >> (3 - b)) & 1 for b in range(4)]
+        num_layers, width = norm_gain.shape
+        hidden_width = w_up.shape[2]
         top_hidden, saved_acts = forward_stack(tokens, norm_gain, w_up, bias_up, w_down, bias_down)
         grad_h = top_gradient(top_hidden, upstream)
-        num_layers = norm_gain.shape[0]
-        reduced = [None] * num_layers
+        smalls, ups, downs = [None] * num_layers, [None] * num_layers, [None] * num_layers
         for layer_idx in reversed(range(num_layers)):
-            local_grads, grad_h = layer_backward(grad_h, saved_acts[layer_idx], norm_gain[layer_idx], w_up[layer_idx], w_down[layer_idx], layer_idx > 0)
-            reduced[layer_idx] = lax.psum(local_grads, data_axis)
-        return tuple(jnp.stack([reduced[layer_idx][which_grad] for layer_idx in range(num_layers)]) for which_grad in range(5))
+            (smalls[layer_idx], ups[layer_idx], downs[layer_idx]), grad_h = layer_backward(
+                grad_h, saved_acts[layer_idx], norm_gain[layer_idx], w_up[layer_idx], w_down[layer_idx], layer_idx > 0,
+                lambda local: reduce_matrix(local, bits, axis),
+            )
+        small = lax.psum(jnp.stack(smalls), axis)
+        up_full = jnp.stack(ups).astype(jnp.float32)
+        down_full = jnp.stack(downs).astype(jnp.float32)
+        return (small[:, :width], up_full, small[:, width:width + hidden_width], down_full, small[:, width + hidden_width:])
 
-    row_spec = P(data_axis, None)
+    row_spec = P(axis, None)
     full_spec = P()
     return jax.shard_map(
         device_grads,

time: 1760 us -> 1020 us (0.58)
  waiting for transfers between devices: 1230 us -> 366 us
  other arithmetic: 116 us -> 172 us
  starting transfers between devices: 0.12 us -> 41.2 us
  local copies, waits for them, and re-layouts: 4.28 us -> 35.2 us
    psum x3 -> x1, waiting for transfers between devices: 1230 us -> 0.02 us  [device_grads(): small = lax.psum(jnp.stack(smalls), axis)]
    ppermute x0 -> x40, waiting for transfers between devices: none -> 322 us  [the longest x36 259 us: reduce_matrix(): received.append((lax.ppermute(sent, axis, flip_pairs(bit)), bit))]
    convert_element_type x0 -> x30, other arithmetic: none -> 132 us  [the longest x28 60.6 us: reduce_matrix(): sent = total(list(starts), list(sizes)).astype(jnp.bfloat16)]
    another operation x4 -> x1, other arithmetic: 101 us -> 0.7 us  [device_grads(): small = lax.psum(jnp.stack(smalls), axis)]
    all_gather x0 -> x4, waiting for transfers between devices: none -> 43.8 us  [reduce_matrix(): return lax.all_gather(shard, axis, tiled=True)]
    ppermute x0 -> x40, starting transfers between devices: none -> 41 us  [the longest x36 40.2 us: reduce_matrix(): received.append((lax.ppermute(sent, axis, flip_pairs(bit)), bit))]
    convert_element_type x0 -> x4, local copies, waits for them, and re-layouts: none -> 31.5 us  [reduce_matrix(): sent = pick(view, starts, sizes).astype(jnp.bfloat16)]
    reshape x0 -> x8, other arithmetic: none -> 19.4 us  [reduce_matrix(): total(list(starts), list(sizes)).astype(jnp.bfloat16).reshape(sub, cols)]
  transfers between devices with their start and end apart: 3 -> 45, of which waited for: 2 -> 30; matrix products, arithmetic and copies ran while one was open for 10% -> 33% of each run, Pallas kernels for 0% -> 0%
where the time goes in v1:
time: 1020 us
  matrix products  389 us (38%)
  waiting for transfers between devices  366 us (36%)
  other arithmetic  172 us (17%)
  starting transfers between devices  41.2 us (4%)
  local copies, waits for them, and re-layouts  35.2 us (3%)
  between operations  14.6 us (1%)
    ppermute x36, waiting for transfers between devices, reduce_matrix(): received.append((lax.ppermute(sent, axis, flip_pairs(bit)), bit))  259 us
    dot_general x2, matrix products, layer_backward(): lax.dot_general(grad_b, down_mat, FEATURE_DIMS, preferred_element_type=jn...  80.9 us
    dot_general x2, matrix products, forward_stack(): jnp.dot(activated, w_down[layer_idx], preferred_element_type=jnp.float32)  74.6 us
    dot_general x2, matrix products, layer_backward(): lax.dot_general(activated, grad_b, TOKEN_DIMS, preferred_element_type=jnp...  69 us
    ppermute x4, waiting for transfers between devices, reduce_matrix(): first = lax.ppermute(sent, axis, flip_pairs(CORE_BIT))  62.8 us
    convert_element_type x28, other arithmetic, reduce_matrix(): sent = total(list(starts), list(sizes)).astype(jnp.bfloat16)  60.6 us
    dot_general x2, matrix products, layer_backward(): lax.dot_general(normed, grad_pre_b, TOKEN_DIMS, preferred_element_type=jn...  56.6 us
    dot_general x2, matrix products, layer_backward(): lax.dot_general(grad_pre_b, up_mat, FEATURE_DIMS, preferred_element_type=...  56.2 us
  transfers between devices with their start and end apart: 45, of which 30 were waited for; matrix products, arithmetic and copies ran while one was open for 33% of the time, Pallas kernels for 0%

profile of v1, /device:TPU:0, one launch (start us, length us, event | category | flops | bytes accessed | tf_op | source)
XLA Modules:
  0.0 1018.0 jit_solution(3444480184599544279)
XLA Ops:
  12.3 26.1 %add_convert_fusion.1 = bf16[1024,6144]{1,0:T(8,128)(2,1)} fusion(f32[6144]{0:T(1024)S(1)} %bitcast.133, bf16[2,1536,6144]{2,1,0:T(8,128)(2,1)} %param.10, bf16[1024,1536]{1,0:T(8,128)(2,1)} %param.7, f32[1536]{0:T(1024)S(1)} %get-tuple-element.8, f32[1024]{0:T(1024)S(1)} %add_rsqrt_fusion.2), kind=kOutput, calls=%fused_computation.31 | convolution fusion | flops 19346227200 | bytes 34637824 | tf_op jit(solution)/shard_map/dot_general | solution.py:29
  38.4 39.5 %fusion.71 = (f32[1024]{0:T(1024)S(1)}, bf16[1024,1536]{1,0:T(8,128)(2,1)}) fusion(f32[1536]{0:T(1024)S(1)} %get-tuple-element.10, bf16[2,6144,1536]{2,1,0:T(8,128)(2,1)} %param.12, bf16[1024,6144]{1,0:T(8,128)(2,1)} %add_convert_fusion.1, bf16[1024,1536]{1,0:T(8,128)(2,1)S(1)} %copy-done.3), kind=kOutput, calls=%fused_computation.91 | convolution fusion | flops 19401277440 | bytes 37758976 | tf_op jit(solution)/shard_map/dot_general | solution.py:31
  78.0 26.0 %add_convert_fusion = bf16[1024,6144]{1,0:T(8,128)(2,1)} fusion(f32[6144]{0:T(1024)S(1)} %bitcast.132, bf16[2,1536,6144]{2,1,0:T(8,128)(2,1)} %param.10, bf16[1024,1536]{1,0:T(8,128)(2,1)} %get-tuple-element.39, f32[1536]{0:T(1024)S(1)} %get-tuple-element.7, f32[1024]{0:T(1024)S(1)} %add_rsqrt_fusion.1), kind=kOutput, calls=%fused_computation.30 | convolution fusion | flops 19346227200 | bytes 34637824 | tf_op jit(solution)/shard_map/dot_general | solution.py:29
  104.0 35.1 %fusion.59 = (f32[1024]{0:T(1024)S(1)}, bf16[1024,1536]{1,0:T(8,128)(2,1)}) fusion(f32[1536]{0:T(1024)S(1)} %get-tuple-element.9, bf16[2,6144,1536]{2,1,0:T(8,128)(2,1)} %param.12, bf16[1024,6144]{1,0:T(8,128)(2,1)} %add_convert_fusion, bf16[1024,1536]{1,0:T(8,128)(2,1)} %get-tuple-element.39), kind=kOutput, calls=%fused_computation.79 | convolution fusion | flops 19401277440 | bytes 37758976 | tf_op jit(solution)/shard_map/dot_general | solution.py:31
  142.2 41.6 %fusion.119 = (f32[6144]{0:T(1024)}, bf16[1024,6144]{1,0:T(8,128)(2,1)}) fusion(bf16[1024,6144]{1,0:T(8,128)(2,1)} %add_convert_fusion, bf16[2,6144,1536]{2,1,0:T(8,128)(2,1)} %param.12, bf16[1024,1536]{1,0:T(8,128)(2,1)} %get-tuple-element.41, bf16[1024,1536]{1,0:T(8,128)(2,1)S(1)} %copy-done, f32[1024]{0:T(1024)S(1)} %broadcast_multiply_fusion.1, ...), kind=kOutput, calls=%fused_computation.186 | convolution fusion | flops 19476768768 | bytes 50364416 | tf_op jit(solution)/shard_map/dot_general | solution.py:97
  183.8 28.8 %fusion.77 = f32[1536,6144]{1,0:T(8,128)} fusion(bf16[1024,6144]{1,0:T(8,128)(2,1)} %get-tuple-element.44, bf16[1024,1536]{1,0:T(8,128)(2,1)} %get-tuple-element.39, f32[1536]{0:T(1024)S(1)} %copy-done.12, f32[1024]{0:T(1024)S(1)} %copy-done.17), kind=kOutput, calls=%fused_computation.97 | convolution fusion | flops 19333644288 | bytes 53487616 | tf_op jit(solution)/shard_map/dot_general | solution.py:101
  223.2 29.3 %fusion.66 = (f32[1024]{0:T(1024)S(1)}, f32[1536]{0:T(1024)S(1)}, f32[1024,1536]{1,0:T(8,128)}) fusion(bf16[1024,1536]{1,0:T(8,128)(2,1)} %get-tuple-element.39, f32[1536]{0:T(1024)S(1)} %copy-done.12, f32[1024]{0:T(1024)S(1)} %copy-done.17, bf16[2,1536,6144]{2,1,0:T(8,128)(2,1)} %param.10, bf16[1024,6144]{1,0:T(8,128)(2,1)} %get-tuple-element.44), kind=kOutput, calls=%fused_computation.86 | convolution fusion | flops 19338360832 | bytes 40914944 | tf_op jit(solution)/shard_map/dot_general | solution.py:103
  277.3 39.3 %fusion.120 = (f32[6144]{0:T(1024)S(1)}, bf16[1024,6144]{1,0:T(8,128)(2,1)}) fusion(bf16[1024,6144]{1,0:T(8,128)(2,1)} %add_convert_fusion.1, bf16[2,6144,1536]{2,1,0:T(8,128)(2,1)} %param.12, bf16[1024,1536]{1,0:T(8,128)(2,1)S(1)} %get-tuple-element.12), kind=kOutput, calls=%fused_computation.187 | convolution fusion | flops 19465758720 | bytes 47210496 | tf_op jit(solution)/shard_map/dot_general | solution.py:97
  324.3 13.8 %collective-permute-done.12 = bf16[2,1,1,1,1,32,6144]{6,5,4,3,2,1,0:T(8,128)(2,1)S(1)} collective-permute-done((bf16[2,1,1,1,1,32,6144]{6,5,4,3,2,1,0:T(8,128)(2,1)S(1)}, bf16[2,1,1,1,1,32,6144]{6,5,4,3,2,1,0:T(8,128)(2,1)S(1)}, u32[]{:S(2)}, u32[]{:S(2)}) %collective-permute-start.12) | collective-permute-done | bytes 786464 | tf_op jit(solution)/shard_map/ppermute | solution.py:85
  340.0 27.0 %fusion.58 = f32[1536]{0:T(1024)S(1)} fusion(bf16[1024,1536]{1,0:T(8,128)(2,1)S(1)} %copy-done.4, f32[1024]{0:T(1024)S(1)} %copy-done.21, bf16[2,1536,6144]{2,1,0:T(8,128)(2,1)} %param.10, bf16[1024,6144]{1,0:T(8,128)(2,1)} %get-tuple-element.46), kind=kOutput, calls=%fused_computation.78 | convolution fusion | flops 19333642240 | bytes 34613248 | tf_op jit(solution)/shard_map/dot_general | solution.py:103
  385.7 27.8 %fusion.74 = f32[1536,6144]{1,0:T(8,128)} fusion(bf16[1024,6144]{1,0:T(8,128)(2,1)} %get-tuple-element.46, bf16[1024,1536]{1,0:T(8,128)(2,1)S(1)} %copy-done.4, f32[1536]{0:T(1024)S(1)} %copy-done.19, f32[1024]{0:T(1024)S(1)} %copy-done.21), kind=kOutput, calls=%fused_computation.94 | convolution fusion | flops 19333644288 | bytes 53487616 | tf_op jit(solution)/shard_map/dot_general | solution.py:101
  420.6 14.7 %collective-permute-done = bf16[2,2,2,1,3,32,6144]{6,5,4,3,2,1,0:T(8,128)(2,1)S(1)} collective-permute-done((bf16[2,2,2,1,3,32,6144]{6,5,4,3,2,1,0:T(8,128)(2,1)S(1)}, bf16[2,2,2,1,3,32,6144]{6,5,4,3,2,1,0:T(8,128)(2,1)S(1)}, u32[]{:S(2)}, u32[]{:S(2)}) %collective-permute-start) | collective-permute-done | bytes 9437216 | tf_op jit(solution)/shard_map/ppermute | solution.py:64
  445.7 46.5 %collective-permute-done.1 = bf16[2,2,1,1,1,32,6144]{6,5,4,3,2,1,0:T(8,128)(2,1)S(1)} collective-permute-done((bf16[2,2,1,1,1,32,6144]{6,5,4,3,2,1,0:T(8,128)(2,1)S(1)}, bf16[2,2,1,1,1,32,6144]{6,5,4,3,2,1,0:T(8,128)(2,1)S(1)}, u32[]{:S(2)}, u32[]{:S(2)}) %collective-permute-start.1) | collective-permute-done | bytes 1572896 | tf_op jit(solution)/shard_map/ppermute | solution.py:85
  509.5 16.0 %collective-permute-done.2 = bf16[2,1,1,1,1,32,6144]{6,5,4,3,2,1,0:T(8,128)(2,1)S(1)} collective-permute-done((bf16[2,1,1,1,1,32,6144]{6,5,4,3,2,1,0:T(8,128)(2,1)S(1)}, bf16[2,1,1,1,1,32,6144]{6,5,4,3,2,1,0:T(8,128)(2,1)S(1)}, u32[]{:S(2)}, u32[]{:S(2)}) %collective-permute-start.2) | collective-permute-done | bytes 786464 | tf_op jit(solution)/shard_map/ppermute | solution.py:85
  567.4 36.8 %fusion.109 = f32[6144,1536]{1,0:T(8,128)} fusion(bf16[1024,6144]{1,0:T(8,128)(2,1)} %add_convert_fusion, bf16[1024,1536]{1,0:T(8,128)(2,1)} %get-tuple-element.41, bf16[1024,1536]{1,0:T(8,128)(2,1)S(1)} %copy-done.1, f32[1024]{0:T(1024)S(1)} %copy-done.15, f32[1024]{0:T(1024)S(1)} %copy-done.10), kind=kOutput, calls=%fused_computation.183 | convolution fusion | flops 19401277440 | bytes 56631296 | tf_op jit(solution)/shard_map/dot_general | solution.py:95
  611.7 24.8 %collective-permute-done.30 = bf16[2,2,2,1,3,128,1536]{6,5,4,3,2,1,0:T(8,128)(2,1)S(1)} collective-permute-done((bf16[2,2,2,1,3,128,1536]{6,5,4,3,2,1,0:T(8,128)(2,1)S(1)}, bf16[2,2,2,1,3,128,1536]{6,5,4,3,2,1,0:T(8,128)(2,1)S(1)}, u32[]{:S(2)}, u32[]{:S(2)}) %collective-permute-start.30) | collective-permute-done | bytes 9437216 | tf_op jit(solution)/shard_map/ppermute | solution.py:64
  647.9 35.3 %collective-permute-done.31 = bf16[2,2,1,1,1,128,1536]{6,5,4,3,2,1,0:T(8,128)(2,1)S(1)} collective-permute-done((bf16[2,2,1,1,1,128,1536]{6,5,4,3,2,1,0:T(8,128)(2,1)S(1)}, bf16[2,2,1,1,1,128,1536]{6,5,4,3,2,1,0:T(8,128)(2,1)S(1)}, u32[]{:S(2)}, u32[]{:S(2)}) %collective-permute-start.31) | collective-permute-done | bytes 1572896 | tf_op jit(solution)/shard_map/ppermute | solution.py:85
  692.0 12.3 %collective-permute-done.32 = bf16[2,1,1,1,1,128,1536]{6,5,4,3,2,1,0:T(8,128)(2,1)S(1)} collective-permute-done((bf16[2,1,1,1,1,128,1536]{6,5,4,3,2,1,0:T(8,128)(2,1)S(1)}, bf16[2,1,1,1,1,128,1536]{6,5,4,3,2,1,0:T(8,128)(2,1)S(1)}, u32[]{:S(2)}, u32[]{:S(2)}) %collective-permute-start.32) | collective-permute-done | bytes 786464 | tf_op jit(solution)/shard_map/ppermute | solution.py:85
  731.6 32.2 %fusion.90 = f32[6144,1536]{1,0:T(8,128)} fusion(bf16[1024,1536]{1,0:T(8,128)(2,1)S(1)} %copy-done.6, bf16[1024,6144]{1,0:T(8,128)(2,1)} %add_convert_fusion.1), kind=kOutput, calls=%fused_computation.126 | convolution fusion | flops 19390267392 | bytes 53477376 | tf_op jit(solution)/shard_map/dot_general | solution.py:95
  771.0 23.4 %collective-permute-done.20 = bf16[2,2,2,1,3,128,1536]{6,5,4,3,2,1,0:T(8,128)(2,1)S(1)} collective-permute-done((bf16[2,2,2,1,3,128,1536]{6,5,4,3,2,1,0:T(8,128)(2,1)S(1)}, bf16[2,2,2,1,3,128,1536]{6,5,4,3,2,1,0:T(8,128)(2,1)S(1)}, u32[]{:S(2)}, u32[]{:S(2)}) %collective-permute-start.20) | collective-permute-done | bytes 9437216 | tf_op jit(solution)/shard_map/ppermute | solution.py:64
  803.8 40.8 %collective-permute-done.21 = bf16[2,2,1,1,1,128,1536]{6,5,4,3,2,1,0:T(8,128)(2,1)S(1)} collective-permute-done((bf16[2,2,1,1,1,128,1536]{6,5,4,3,2,1,0:T(8,128)(2,1)S(1)}, bf16[2,2,1,1,1,128,1536]{6,5,4,3,2,1,0:T(8,128)(2,1)S(1)}, u32[]{:S(2)}, u32[]{:S(2)}) %collective-permute-start.21) | collective-permute-done | bytes 1572896 | tf_op jit(solution)/shard_map/ppermute | solution.py:85
  895.6 35.7 %maximum_convert_fusion = f32[2,1536,6144]{2,1,0:T(8,128)} fusion(bf16[1,1536,6144]{2,1,0:T(8,128)(2,1)} %bitcast.126, bf16[1,1536,6144]{2,1,0:T(8,128)(2,1)} %bitcast.127), kind=kLoop, calls=%fused_computation.10 | loop fusion | flops 37748736 | bytes 113246208 | tf_op jit(solution)/shard_map/convert_element_type | solution.py:130
  931.3 43.8 %all-gather.9.cloned.1.call-done = bf16[6144,1536]{1,0:T(8,128)(2,1)} async-done(((bf16[384,1536]{1,0:T(8,128)(2,1)}), bf16[6144,1536]{1,0:T(8,128)(2,1)}) %all-gather.9.cloned.1.call-update) | async-done | bytes 18874384 | tf_op jit(solution)/shard_map/all_gather | solution.py:89
  975.1 36.1 %maximum_convert_fusion.1 = f32[2,6144,1536]{2,1,0:T(8,128)} fusion(bf16[1,6144,1536]{2,1,0:T(8,128)(2,1)} %bitcast.128, bf16[1,6144,1536]{2,1,0:T(8,128)(2,1)} %bitcast.129), kind=kLoop, calls=%fused_computation.11 | loop fusion | flops 37748736 | bytes 113246208 | tf_op jit(solution)/shard_map/convert_element_type | solution.py:131
  (188 shorter events, 270.9 us)
Async XLA Ops:
  7.2 885.6 %all-reduce.2.cloned.1.call-start = ((), (), s32[]{:S(2)}) async-start(), calls=%async_computation | async-start | bytes 147456 | tf_op jit(solution)/shard_map/psum | solution.py:129
  222.5 36.6 %collective-permute-start.10 = (bf16[2,2,2,1,3,32,6144]{6,5,4,3,2,1,0:T(8,128)(2,1)}, bf16[2,2,2,1,3,32,6144]{6,5,4,3,2,1,0:T(8,128)(2,1)}, u32[]{:S(2)}, u32[]{:S(2)}) collective-permute-start(bf16[2,2,2,1,3,32,6144]{6,5,4,3,2,1,0:T(8,128)(2,1)} %dynamic-slice_convert_fusion.2), channel_id=1, source_target_pairs={{0,1},{1,0},{2,3},{3,2},{4,5},{5,4},{6,7},{7,6},{8,9},{9,8},{10,11... | collective-permute-start | bytes 28311560 | tf_op jit(solution)/shard_map/ppermute | solution.py:64
  264.1 52.6 %collective-permute-start.11 = (bf16[2,2,1,1,1,32,6144]{6,5,4,3,2,1,0:T(8,128)(2,1)}, bf16[2,2,1,1,1,32,6144]{6,5,4,3,2,1,0:T(8,128)(2,1)}, u32[]{:S(2)}, u32[]{:S(2)}) collective-permute-start(bf16[2,2,1,1,1,32,6144]{6,5,4,3,2,1,0:T(8,128)(2,1)} %add_convert_fusion.10), channel_id=1, source_target_pairs={{0,2},{1,3},{2,0},{3,1},{4,6},{5,7},{6,4},{7,5},{8,10},{9,11},{10,... | collective-permute-start | bytes 4718600 | tf_op jit(solution)/shard_map/ppermute | solution.py:85
  270.4 49.0 %collective-permute-start.14 = (bf16[2,1,2,1,1,32,6144]{6,5,4,3,2,1,0:T(8,128)(2,1)}, bf16[2,1,2,1,1,32,6144]{6,5,4,3,2,1,0:T(8,128)(2,1)}, u32[]{:S(2)}, u32[]{:S(2)}) collective-permute-start(bf16[2,1,2,1,1,32,6144]{6,5,4,3,2,1,0:T(8,128)(2,1)} %add_convert_fusion.9), channel_id=1, source_target_pairs={{0,4},{1,5},{2,6},{3,7},{4,0},{5,1},{6,2},{7,3},{8,12},{9,13},{10,... | collective-permute-start | bytes 4718600 | tf_op jit(solution)/shard_map/ppermute | solution.py:85
  275.8 46.3 %collective-permute-start.17 = (bf16[1,2,2,1,1,32,6144]{6,5,4,3,2,1,0:T(8,128)(2,1)}, bf16[1,2,2,1,1,32,6144]{6,5,4,3,2,1,0:T(8,128)(2,1)}, u32[]{:S(2)}, u32[]{:S(2)}) collective-permute-start(bf16[1,2,2,1,1,32,6144]{6,5,4,3,2,1,0:T(8,128)(2,1)} %add_convert_fusion.8), channel_id=1, source_target_pairs={{0,8},{1,9},{2,10},{3,11},{4,12},{5,13},{6,14},{7,15},{8,0},{9,1},... | collective-permute-start | bytes 4718600 | tf_op jit(solution)/shard_map/ppermute | solution.py:85
  321.5 45.5 %collective-permute-start.15 = (bf16[1,1,2,1,1,32,6144]{6,5,4,3,2,1,0:T(8,128)(2,1)S(1)}, bf16[1,1,2,1,1,32,6144]{6,5,4,3,2,1,0:T(8,128)(2,1)S(1)}, u32[]{:S(2)}, u32[]{:S(2)}) collective-permute-start(bf16[1,1,2,1,1,32,6144]{6,5,4,3,2,1,0:T(8,128)(2,1)S(1)} %add_convert_fusion.21), channel_id=1, source_target_pairs={{0,8},{1,9},{2,10},{3,11},{4,12},{5,13},{6,14},{7,15},{8,0},{9,1},... | collective-permute-start | bytes 2359304 | tf_op jit(solution)/shard_map/ppermute | solution.py:85
  324.1 43.0 %collective-permute-start.18 = (bf16[1,2,1,1,1,32,6144]{6,5,4,3,2,1,0:T(8,128)(2,1)S(1)}, bf16[1,2,1,1,1,32,6144]{6,5,4,3,2,1,0:T(8,128)(2,1)S(1)}, u32[]{:S(2)}, u32[]{:S(2)}) collective-permute-start(bf16[1,2,1,1,1,32,6144]{6,5,4,3,2,1,0:T(8,128)(2,1)S(1)} %add_convert_fusion.20), channel_id=1, source_target_pairs={{0,2},{1,3},{2,0},{3,1},{4,6},{5,7},{6,4},{7,5},{8,10},{9,11},{10,... | collective-permute-start | bytes 2359304 | tf_op jit(solution)/shard_map/ppermute | solution.py:85
  339.6 27.5 %collective-permute-start.13 = (bf16[1,1,1,1,1,32,6144]{6,5,4,3,2,1,0:T(8,128)(2,1)S(1)}, bf16[1,1,1,1,1,32,6144]{6,5,4,3,2,1,0:T(8,128)(2,1)S(1)}, u32[]{:S(2)}, u32[]{:S(2)}) collective-permute-start(bf16[1,1,1,1,1,32,6144]{6,5,4,3,2,1,0:T(8,128)(2,1)S(1)} %add_convert_fusion.43), channel_id=1, source_target_pairs={{0,8},{1,9},{2,10},{3,11},{4,12},{5,13},{6,14},{7,15},{8,0},{9,1},... | collective-permute-start | bytes 1179656 | tf_op jit(solution)/shard_map/ppermute | solution.py:85
  373.5 522.1 %all-gather.7.cloned.1.call-start = ((), (), s32[]{:S(2)}) async-start(), calls=%async_computation.2 | async-start | bytes 20054016 | tf_op jit(solution)/shard_map/all_gather | solution.py:89
  385.6 509.9 %all-gather.5.cloned.1.call-start = ((), (), s32[]{:S(2)}) async-start(), calls=%async_computation.1 | async-start | bytes 20054016 | tf_op jit(solution)/shard_map/all_gather | solution.py:89
  437.5 54.7 %collective-permute-start.1 = (bf16[2,2,1,1,1,32,6144]{6,5,4,3,2,1,0:T(8,128)(2,1)S(1)}, bf16[2,2,1,1,1,32,6144]{6,5,4,3,2,1,0:T(8,128)(2,1)S(1)}, u32[]{:S(2)}, u32[]{:S(2)}) collective-permute-start(bf16[2,2,1,1,1,32,6144]{6,5,4,3,2,1,0:T(8,128)(2,1)S(1)} %add_convert_fusion.13), channel_id=1, source_target_pairs={{0,2},{1,3},{2,0},{3,1},{4,6},{5,7},{6,4},{7,5},{8,10},{9,11},{10,... | collective-permute-start | bytes 4718600 | tf_op jit(solution)/shard_map/ppermute | solution.py:85
  440.4 58.5 %collective-permute-start.4 = (bf16[2,1,2,1,1,32,6144]{6,5,4,3,2,1,0:T(8,128)(2,1)S(1)}, bf16[2,1,2,1,1,32,6144]{6,5,4,3,2,1,0:T(8,128)(2,1)S(1)}, u32[]{:S(2)}, u32[]{:S(2)}) collective-permute-start(bf16[2,1,2,1,1,32,6144]{6,5,4,3,2,1,0:T(8,128)(2,1)S(1)} %add_convert_fusion.12), channel_id=1, source_target_pairs={{0,4},{1,5},{2,6},{3,7},{4,0},{5,1},{6,2},{7,3},{8,12},{9,13},{10,... | collective-permute-start | bytes 4718600 | tf_op jit(solution)/shard_map/ppermute | solution.py:85
  444.1 62.1 %collective-permute-start.7 = (bf16[1,2,2,1,1,32,6144]{6,5,4,3,2,1,0:T(8,128)(2,1)S(1)}, bf16[1,2,2,1,1,32,6144]{6,5,4,3,2,1,0:T(8,128)(2,1)S(1)}, u32[]{:S(2)}, u32[]{:S(2)}) collective-permute-start(bf16[1,2,2,1,1,32,6144]{6,5,4,3,2,1,0:T(8,128)(2,1)S(1)} %add_convert_fusion.11), channel_id=1, source_target_pairs={{0,8},{1,9},{2,10},{3,11},{4,12},{5,13},{6,14},{7,15},{8,0},{9,1},... | collective-permute-start | bytes 4718600 | tf_op jit(solution)/shard_map/ppermute | solution.py:85
  493.9 31.5 %collective-permute-start.2 = (bf16[2,1,1,1,1,32,6144]{6,5,4,3,2,1,0:T(8,128)(2,1)S(1)}, bf16[2,1,1,1,1,32,6144]{6,5,4,3,2,1,0:T(8,128)(2,1)S(1)}, u32[]{:S(2)}, u32[]{:S(2)}) collective-permute-start(bf16[2,1,1,1,1,32,6144]{6,5,4,3,2,1,0:T(8,128)(2,1)S(1)} %add_convert_fusion.25), channel_id=1, source_target_pairs={{0,4},{1,5},{2,6},{3,7},{4,0},{5,1},{6,2},{7,3},{8,12},{9,13},{10,... | collective-permute-start | bytes 2359304 | tf_op jit(solution)/shard_map/ppermute | solution.py:85
  500.6 33.7 %collective-permute-start.5 = (bf16[1,1,2,1,1,32,6144]{6,5,4,3,2,1,0:T(8,128)(2,1)S(1)}, bf16[1,1,2,1,1,32,6144]{6,5,4,3,2,1,0:T(8,128)(2,1)S(1)}, u32[]{:S(2)}, u32[]{:S(2)}) collective-permute-start(bf16[1,1,2,1,1,32,6144]{6,5,4,3,2,1,0:T(8,128)(2,1)S(1)} %add_convert_fusion.24), channel_id=1, source_target_pairs={{0,8},{1,9},{2,10},{3,11},{4,12},{5,13},{6,14},{7,15},{8,0},{9,1},... | collective-permute-start | bytes 2359304 | tf_op jit(solution)/shard_map/ppermute | solution.py:85
  507.9 29.6 %collective-permute-start.8 = (bf16[1,2,1,1,1,32,6144]{6,5,4,3,2,1,0:T(8,128)(2,1)S(1)}, bf16[1,2,1,1,1,32,6144]{6,5,4,3,2,1,0:T(8,128)(2,1)S(1)}, u32[]{:S(2)}, u32[]{:S(2)}) collective-permute-start(bf16[1,2,1,1,1,32,6144]{6,5,4,3,2,1,0:T(8,128)(2,1)S(1)} %add_convert_fusion.23), channel_id=1, source_target_pairs={{0,2},{1,3},{2,0},{3,1},{4,6},{5,7},{6,4},{7,5},{8,10},{9,11},{10,... | collective-permute-start | bytes 2359304 | tf_op jit(solution)/shard_map/ppermute | solution.py:85
  567.4 364.0 %all-gather.11.cloned.1.call-start = ((), (), s32[]{:S(2)}) async-start(), calls=%async_computation.4 | async-start | bytes 20054016 | tf_op jit(solution)/shard_map/all_gather | solution.py:89
  638.8 44.4 %collective-permute-start.31 = (bf16[2,2,1,1,1,128,1536]{6,5,4,3,2,1,0:T(8,128)(2,1)S(1)}, bf16[2,2,1,1,1,128,1536]{6,5,4,3,2,1,0:T(8,128)(2,1)S(1)}, u32[]{:S(2)}, u32[]{:S(2)}) collective-permute-start(bf16[2,2,1,1,1,128,1536]{6,5,4,3,2,1,0:T(8,128)(2,1)S(1)} %add_convert_fusion.4), channel_id=1, source_target_pairs={{0,2},{1,3},{2,0},{3,1},{4,6},{5,7},{6,4},{7,5},{8,10},{9,11},{10,... | collective-permute-start | bytes 4718600 | tf_op jit(solution)/shard_map/ppermute | solution.py:85
  642.6 43.9 %collective-permute-start.34 = (bf16[2,1,2,1,1,128,1536]{6,5,4,3,2,1,0:T(8,128)(2,1)S(1)}, bf16[2,1,2,1,1,128,1536]{6,5,4,3,2,1,0:T(8,128)(2,1)S(1)}, u32[]{:S(2)}, u32[]{:S(2)}) collective-permute-start(bf16[2,1,2,1,1,128,1536]{6,5,4,3,2,1,0:T(8,128)(2,1)S(1)} %add_convert_fusion.3), channel_id=1, source_target_pairs={{0,4},{1,5},{2,6},{3,7},{4,0},{5,1},{6,2},{7,3},{8,12},{9,13},{10,... | collective-permute-start | bytes 4718600 | tf_op jit(solution)/shard_map/ppermute | solution.py:85
  645.0 44.7 %collective-permute-start.37 = (bf16[1,2,2,1,1,128,1536]{6,5,4,3,2,1,0:T(8,128)(2,1)S(1)}, bf16[1,2,2,1,1,128,1536]{6,5,4,3,2,1,0:T(8,128)(2,1)S(1)}, u32[]{:S(2)}, u32[]{:S(2)}) collective-permute-start(bf16[1,2,2,1,1,128,1536]{6,5,4,3,2,1,0:T(8,128)(2,1)S(1)} %add_convert_fusion.2), channel_id=1, source_target_pairs={{0,8},{1,9},{2,10},{3,11},{4,12},{5,13},{6,14},{7,15},{8,0},{9,1},... | collective-permute-start | bytes 4718600 | tf_op jit(solution)/shard_map/ppermute | solution.py:85
  731.5 243.6 %all-gather.9.cloned.1.call-start = ((), (), s32[]{:S(2)}) async-start(), calls=%async_computation.3 | async-start | bytes 20054016 | tf_op jit(solution)/shard_map/all_gather | solution.py:89
  796.7 47.9 %collective-permute-start.21 = (bf16[2,2,1,1,1,128,1536]{6,5,4,3,2,1,0:T(8,128)(2,1)S(1)}, bf16[2,2,1,1,1,128,1536]{6,5,4,3,2,1,0:T(8,128)(2,1)S(1)}, u32[]{:S(2)}, u32[]{:S(2)}) collective-permute-start(bf16[2,2,1,1,1,128,1536]{6,5,4,3,2,1,0:T(8,128)(2,1)S(1)} %add_convert_fusion.7), channel_id=1, source_target_pairs={{0,2},{1,3},{2,0},{3,1},{4,6},{5,7},{6,4},{7,5},{8,10},{9,11},{10,... | collective-permute-start | bytes 4718600 | tf_op jit(solution)/shard_map/ppermute | solution.py:85
  799.7 48.1 %collective-permute-start.24 = (bf16[2,1,2,1,1,128,1536]{6,5,4,3,2,1,0:T(8,128)(2,1)S(1)}, bf16[2,1,2,1,1,128,1536]{6,5,4,3,2,1,0:T(8,128)(2,1)S(1)}, u32[]{:S(2)}, u32[]{:S(2)}) collective-permute-start(bf16[2,1,2,1,1,128,1536]{6,5,4,3,2,1,0:T(8,128)(2,1)S(1)} %add_convert_fusion.6), channel_id=1, source_target_pairs={{0,4},{1,5},{2,6},{3,7},{4,0},{5,1},{6,2},{7,3},{8,12},{9,13},{10,... | collective-permute-start | bytes 4718600 | tf_op jit(solution)/shard_map/ppermute | solution.py:85
  802.7 48.4 %collective-permute-start.27 = (bf16[1,2,2,1,1,128,1536]{6,5,4,3,2,1,0:T(8,128)(2,1)S(1)}, bf16[1,2,2,1,1,128,1536]{6,5,4,3,2,1,0:T(8,128)(2,1)S(1)}, u32[]{:S(2)}, u32[]{:S(2)}) collective-permute-start(bf16[1,2,2,1,1,128,1536]{6,5,4,3,2,1,0:T(8,128)(2,1)S(1)} %add_convert_fusion.5), channel_id=1, source_target_pairs={{0,8},{1,9},{2,10},{3,11},{4,12},{5,13},{6,14},{7,15},{8,0},{9,1},... | collective-permute-start | bytes 4718600 | tf_op jit(solution)/shard_map/ppermute | solution.py:85
  (43 other events, 1034.3 us)
Sparse Core Ops, SparseCore 0:
  373.6 66.1 all-reduce.1
  442.0 124.8 all-gather.6
  569.2 90.5 all-gather.4
  731.6 93.0 all-gather.10
  892.9 82.1 all-gather.8

commit v2 on v0

--- a/solution.py
+++ b/solution.py
@@ -1,11 +1,27 @@
+import functools
+
 import jax
 import jax.numpy as jnp
 from jax import lax
+from jax.experimental import pallas as pl
+from jax.experimental.pallas import tpu as pltpu
 from jax.sharding import PartitionSpec as P
 
 EPSILON = 1e-6
 TOKEN_DIMS = (((0,), (0,)), ((), ()))
 FEATURE_DIMS = (((1,), (1,)), ((), ()))
+MESH = pl.DeviceIdType.MESH
+COLORS = 3
+CORE, DIM_X, DIM_Y, DIM_Z = range(4)
+COLOR_DIMS = ((DIM_X, DIM_Y, DIM_Z), (DIM_Y, DIM_Z, DIM_X), (DIM_Z, DIM_X, DIM_Y))
+PIPELINE = (
+    ("load", 0), ("compute_sent", 0), ("compute_kept", 0), ("send_2", 1), ("send_back_3", 2), ("send_back_core", 4),
+    ("send_1", 0), ("send_back_1", 3), ("send_3", 1), ("send_back_2", 2), ("store", 4),
+)
+MAX_LAG = 4
+RECV_SLOTS = 3
+KEPT_SLOTS = 3
+GATHER_SLOTS = 6
 
 
 def gelu_tanh(values):
@@ -42,38 +58,331 @@
 def layer_backward(grad_h, saved_layer, gain_row, up_mat, down_mat, need_input):
     hid_scale, hid_hat, normed, pre_act, activated = saved_layer
     grad_b = grad_h.astype(jnp.bfloat16)
-    grad_down = lax.dot_general(activated, grad_b, TOKEN_DIMS, preferred_element_type=jnp.float32)
     grad_down_bias = jnp.sum(grad_h, axis=0)
     grad_act = lax.dot_general(grad_b, down_mat, FEATURE_DIMS, preferred_element_type=jnp.float32)
     gelu_back = jax.vjp(gelu_tanh, pre_act.astype(jnp.float32))[1]
     grad_pre = gelu_back(grad_act)[0]
     grad_pre_b = grad_pre.astype(jnp.bfloat16)
-    grad_up = lax.dot_general(normed, grad_pre_b, TOKEN_DIMS, preferred_element_type=jnp.float32)
     grad_up_bias = jnp.sum(grad_pre, axis=0)
     grad_normed = lax.dot_general(grad_pre_b, up_mat, FEATURE_DIMS, preferred_element_type=jnp.float32)
     grad_gain = jnp.sum(grad_normed * hid_hat, axis=0)
-    layer_grads = (grad_gain, grad_up, grad_up_bias, grad_down, grad_down_bias)
+    small = jnp.concatenate([grad_gain, grad_up_bias, grad_down_bias])
+    operands = ((activated, grad_b), (normed, grad_pre_b))
     if not need_input:
-        return layer_grads, None
+        return small, operands, None
     grad_hat = grad_normed * gain_row.astype(jnp.float32)
     grad_new = grad_h + hid_scale * (grad_hat - hid_hat * jnp.mean(grad_hat * hid_hat, axis=-1, keepdims=True))
-    return layer_grads, grad_new
+    return small, operands, grad_new
+
+
+def exchange_kernel(sizes, *refs):
+    num_mats, chunks_per_mat, row_dim, chunk_cols, region, down_subs, axis = sizes
+    mats = [(refs[2 * m], refs[2 * m + 1]) for m in range(num_mats)]
+    refs = refs[2 * num_mats:]
+    small_in, gathered, small_out = refs[:3]
+    (rows_buf, cols_buf, sent_core, kept, recv_core, sent_1, sent_2, sent_3, recv_1, recv_2, recv_3, ring,
+     small_recv, load_sem, core_send, core_recv, out_send, out_recv, back_send, back_recv, share_send, share_recv,
+     store_sem, small_send_sem, small_recv_sem) = refs[3:]
+    num_chunks = num_mats * chunks_per_mat
+    half = COLORS * region
+    me = lax.axis_index(axis)
+    bits = [me % 2, (me // 2) % 2, (me // 4) % 2, me // 8]
+    partners = [me + (1 << d) - 2 * (1 << d) * bits[d] for d in range(4)]
+    core = bits[CORE]
+    sent_bufs, recv_bufs = (sent_1, sent_2, sent_3), (recv_1, recv_2, recv_3)
+    spans = (region // 2, region // 4, region // 8)
+
+    def base(color, level):
+        total = 0
+        for step in range(level):
+            total = total + bits[COLOR_DIMS[color][step]] * spans[step]
+        return total
+
+    def other(color, level):
+        return base(color, level) + (1 - bits[COLOR_DIMS[color][level]]) * spans[level]
+
+    def rows_at(start, size):
+        return pl.ds(pl.multiple_of(start, spans[2]), size)
+
+    def load_copies(mat, chunk):
+        slot = chunk % 2
+        sub = chunk % chunks_per_mat
+        rows_ref, cols_ref = mats[mat]
+        if mat % 2 == 0:
+            row_start = pl.multiple_of((sub // down_subs) * row_dim, 128)
+            col_start = pl.multiple_of((sub % down_subs) * chunk_cols, 128)
+            rows_src = rows_ref.at[:, pl.ds(row_start, row_dim)]
+            cols_src = cols_ref.at[:, pl.ds(col_start, chunk_cols)]
+        else:
+            rows_src = rows_ref
+            cols_src = cols_ref.at[:, pl.ds(pl.multiple_of(sub * chunk_cols, 128), chunk_cols)]
+        return (
+            pltpu.make_async_copy(rows_src, rows_buf.at[slot], load_sem.at[0, slot]),
+            pltpu.make_async_copy(cols_src, cols_buf.at[slot], load_sem.at[1, slot]),
+        )
+
+    def start_loads(chunk):
+        for mat in range(num_mats):
+            @pl.when(chunk // chunks_per_mat == mat)
+            def _():
+                for copy in load_copies(mat, chunk):
+                    copy.start()
+
+    def core_copy(chunk):
+        slot = chunk % RECV_SLOTS
+        return pltpu.make_async_remote_copy(
+            src_ref=sent_core, dst_ref=recv_core.at[slot], send_sem=core_send, recv_sem=core_recv.at[slot],
+            device_id=(partners[CORE],), device_id_type=MESH)
+
+    def out_copy(level, color, chunk):
+        slot = chunk % RECV_SLOTS
+        return pltpu.make_async_remote_copy(
+            src_ref=sent_bufs[level].at[color], dst_ref=recv_bufs[level].at[slot, color],
+            send_sem=out_send.at[level, color], recv_sem=out_recv.at[level, color, slot],
+            device_id=(partners[COLOR_DIMS[color][level]],), device_id_type=MESH)
+
+    def back_copy(level, color, chunk, arriving):
+        slot = chunk % GATHER_SLOTS
+        mine = ring.at[slot, core, color, rows_at(base(color, level + 1), spans[level]), :]
+        theirs = ring.at[slot, core, color, rows_at(other(color, level), spans[level]), :]
+        return pltpu.make_async_remote_copy(
+            src_ref=mine, dst_ref=theirs if arriving else mine,
+            send_sem=back_send.at[level, color, slot], recv_sem=back_recv.at[level, color, slot],
+            device_id=(partners[COLOR_DIMS[color][level]],), device_id_type=MESH)
+
+    def share_copy(chunk, arriving):
+        slot = chunk % GATHER_SLOTS
+        return pltpu.make_async_remote_copy(
+            src_ref=ring.at[slot, core], dst_ref=ring.at[slot, 1 - core if arriving else core],
+            send_sem=share_send.at[slot], recv_sem=share_recv.at[slot],
+            device_id=(partners[CORE],), device_id_type=MESH)
+
+    def store_copy(chunk):
+        slot = chunk % GATHER_SLOTS
+        return pltpu.make_async_copy(ring.at[slot], gathered.at[chunk], store_sem.at[slot])
+
+    def small_copy(step):
+        return pltpu.make_async_remote_copy(
+            src_ref=small_out, dst_ref=small_recv.at[step], send_sem=small_send_sem.at[step],
+            recv_sem=small_recv_sem.at[step], device_id=(partners[step],), device_id_type=MESH)
+
+    def product(chunk, which_core, color):
+        slot = chunk % 2
+        start = pl.multiple_of(which_core * half + color * region, 128)
+        return lax.dot_general(
+            rows_buf[slot, :, pl.ds(start, region)], cols_buf[slot], TOKEN_DIMS, preferred_element_type=jnp.float32)
+
+    def load(chunk):
+        for copy in load_copies(1, chunk):
+            copy.wait()
+
+        @pl.when(chunk + 1 < num_chunks)
+        def _():
+            start_loads(chunk + 1)
+
+    def compute_sent(chunk):
+        @pl.loop(0, COLORS)
+        def _(color):
+            sent_core[color] = product(chunk, 1 - core, color).astype(jnp.bfloat16)
+        core_copy(chunk).start()
+
+    def compute_kept(chunk):
+        slot = chunk % KEPT_SLOTS
+
+        @pl.loop(0, COLORS)
+        def _(color):
+            kept[slot, color] = product(chunk, core, color)
+
+    def halve(level, chunk, arrived):
+        slot = chunk % KEPT_SLOTS
+        recv_slot = chunk % RECV_SLOTS
+        for color in range(COLORS):
+            if level > 0:
+                out_copy(level - 1, color, chunk).wait()
+            held = base(color, level)
+
+            def total(start, size, color=color, held=held):
+                own = kept[slot, color, rows_at(start, size), :]
+                return own + arrived[recv_slot, color, rows_at(start - held, size), :].astype(jnp.float32)
+
+            if level < 3:
+                mine = base(color, level + 1)
+                sent_bufs[level][color] = total(other(color, level), spans[level]).astype(jnp.bfloat16)
+                kept[slot, color, rows_at(mine, spans[level]), :] = total(mine, spans[level])
+                out_copy(level, color, chunk).start()
+            else:
+                gather_slot = chunk % GATHER_SLOTS
+                ring[gather_slot, core, color, rows_at(held, spans[2]), :] = total(held, spans[2]).astype(jnp.bfloat16)
+                back_copy(2, color, chunk, False).start()
+
+    def send_1(chunk):
+        core_copy(chunk).wait()
+        halve(0, chunk, recv_core)
+
+    def send_2(chunk):
+        halve(1, chunk, recv_1)
+
+    def send_3(chunk):
+        halve(2, chunk, recv_2)
+
+    def send_back_3(chunk):
+        halve(3, chunk, recv_3)
+
+    def pass_back(level, chunk):
+        for color in range(COLORS):
+            back_copy(level + 1, color, chunk, True).wait()
+            back_copy(level, color, chunk, False).start()
+
+    def send_back_2(chunk):
+        pass_back(1, chunk)
+
+    def send_back_1(chunk):
+        pass_back(0, chunk)
+
+    def send_back_core(chunk):
+        for color in range(COLORS):
+            back_copy(0, color, chunk, True).wait()
+        share_copy(chunk, False).start()
+
+    def store(chunk):
+        share_copy(chunk, True).wait()
+        store_copy(chunk).start()
+
+        @pl.when(chunk > 0)
+        def _():
+            store_copy(chunk - 1).wait()
+
+    events = dict(
+        load=load, compute_sent=compute_sent, compute_kept=compute_kept, send_1=send_1, send_2=send_2, send_3=send_3,
+        send_back_3=send_back_3, send_back_2=send_back_2, send_back_1=send_back_1, send_back_core=send_back_core, store=store)
+
+    start_loads(jnp.int32(0))
+    barrier = pltpu.get_barrier_semaphore()
+    for partner in partners:
+        pl.semaphore_signal(barrier, inc=1, device_id=(partner,), device_id_type=MESH)
+    small_out[...] = small_in[...]
+    pl.semaphore_wait(barrier, 4)
+
+    @pl.loop(0, num_chunks + MAX_LAG)
+    def _(it):
+        for name, lag in PIPELINE:
+            chunk = it - lag
+
+            @pl.when((chunk >= 0) & (chunk < num_chunks))
+            def _(name=name, chunk=chunk):
+                events[name](chunk)
+        for step in range(4):
+            @pl.when(it == 2 * step + 1)
+            def _(step=step):
+                small_copy(step).start()
+
+            @pl.when(it == 2 * step + 2)
+            def _(step=step):
+                small_copy(step).wait()
+                small_out[...] += small_recv[step]
+
+    store_copy(jnp.int32(num_chunks - 1)).wait()
+
+
+def exchange(mat_operands, small, axis, chunk_cols):
+    tokens, row_dim = mat_operands[1][0].shape
+    hidden = mat_operands[0][0].shape[1]
+    num_mats = len(mat_operands)
+    chunks_per_mat = hidden // chunk_cols
+    region = row_dim // (2 * COLORS)
+    half = (COLORS, region, chunk_cols)
+    sizes = (num_mats, chunks_per_mat, row_dim, chunk_cols, region, row_dim // chunk_cols, axis)
+    num_chunks = num_mats * chunks_per_mat
+    small_rows = small.shape[0] // 128
+    bf16, f32 = jnp.bfloat16, jnp.float32
+    dma = pltpu.SemaphoreType.DMA
+    any_spec = pl.BlockSpec(memory_space=pl.ANY)
+    vmem_spec = pl.BlockSpec(memory_space=pltpu.VMEM)
+    gathered, small_sum = pl.pallas_call(
+        functools.partial(exchange_kernel, sizes),
+        out_shape=(
+            jax.ShapeDtypeStruct((num_chunks, 2) + half, bf16),
+            jax.ShapeDtypeStruct((small_rows, 128), f32),
+        ),
+        in_specs=[any_spec] * (2 * num_mats) + [vmem_spec],
+        out_specs=(any_spec, vmem_spec),
+        scratch_shapes=[
+            pltpu.VMEM((2, tokens, row_dim), bf16),
+            pltpu.VMEM((2, tokens, chunk_cols), bf16),
+            pltpu.VMEM(half, bf16),
+            pltpu.VMEM((KEPT_SLOTS,) + half, f32),
+            pltpu.VMEM((RECV_SLOTS,) + half, bf16),
+            pltpu.VMEM((COLORS, region // 2, chunk_cols), bf16),
+            pltpu.VMEM((COLORS, region // 4, chunk_cols), bf16),
+            pltpu.VMEM((COLORS, region // 8, chunk_cols), bf16),
+            pltpu.VMEM((RECV_SLOTS, COLORS, region // 2, chunk_cols), bf16),
+            pltpu.VMEM((RECV_SLOTS, COLORS, region // 4, chunk_cols), bf16),
+            pltpu.VMEM((RECV_SLOTS, COLORS, region // 8, chunk_cols), bf16),
+            pltpu.VMEM((GATHER_SLOTS, 2) + half, bf16),
+            pltpu.VMEM((4, small_rows, 128), f32),
+            dma((2, 2)), dma, dma((RECV_SLOTS,)), dma((3, COLORS)), dma((3, COLORS, RECV_SLOTS)),
+            dma((3, COLORS, GATHER_SLOTS)), dma((3, COLORS, GATHER_SLOTS)), dma((GATHER_SLOTS,)), dma((GATHER_SLOTS,)),
+            dma((GATHER_SLOTS,)), dma((4,)), dma((4,)),
+        ],
+        compiler_params=pltpu.CompilerParams(collective_id=0, has_side_effects=True, vmem_limit_bytes=60 * 2**20),
+        name="exchange",
+    )(*[operand for pair in mat_operands for operand in pair], small.reshape(small_rows, 128))
+    return gathered, small_sum.reshape(-1)
+
+
+def widen_kernel(chunk_ref, out_ref):
+    out_ref[0] = chunk_ref[0].astype(jnp.float32)
+
+
+def widen(gathered, num_layers, row_dim, hidden, chunk_cols):
+    per_mat = hidden // chunk_cols
+    num_mats = 2 * num_layers
+    down_subs = row_dim // chunk_cols
+    chunks = gathered.reshape(num_mats * per_mat, row_dim, chunk_cols)
+
+    def mat_of(layer, kind):
+        return (num_layers - 1 - layer) * 2 + kind
+
+    block = (1, row_dim, chunk_cols)
+    up = pl.pallas_call(
+        widen_kernel,
+        grid=(num_layers, per_mat),
+        in_specs=[pl.BlockSpec(block, lambda layer, sub: (mat_of(layer, 1) * per_mat + sub, 0, 0))],
+        out_specs=pl.BlockSpec(block, lambda layer, sub: (layer, 0, sub)),
+        out_shape=jax.ShapeDtypeStruct((num_layers, row_dim, hidden), jnp.float32),
+        name="widen_up",
+    )(chunks)
+    down = pl.pallas_call(
+        widen_kernel,
+        grid=(num_layers, per_mat),
+        in_specs=[pl.BlockSpec(block, lambda layer, sub: (mat_of(layer, 0) * per_mat + sub, 0, 0))],
+        out_specs=pl.BlockSpec(block, lambda layer, sub: (layer, sub // down_subs, sub % down_subs)),
+        out_shape=jax.ShapeDtypeStruct((num_layers, hidden, row_dim), jnp.float32),
+        name="widen_down",
+    )(chunks)
+    return up, down
 
 
 def solution(mesh):
-    data_axis = mesh.axis_names[0]
+    axis = mesh.axis_names[0]
 
     def device_grads(tokens, upstream, norm_gain, w_up, bias_up, w_down, bias_down):
+        num_layers, width = norm_gain.shape
+        hidden_width = w_up.shape[2]
+        chunk_cols = width // 2
         top_hidden, saved_acts = forward_stack(tokens, norm_gain, w_up, bias_up, w_down, bias_down)
         grad_h = top_gradient(top_hidden, upstream)
-        num_layers = norm_gain.shape[0]
-        reduced = [None] * num_layers
+        smalls, mat_operands = [None] * num_layers, []
         for layer_idx in reversed(range(num_layers)):
-            local_grads, grad_h = layer_backward(grad_h, saved_acts[layer_idx], norm_gain[layer_idx], w_up[layer_idx], w_down[layer_idx], layer_idx > 0)
-            reduced[layer_idx] = lax.psum(local_grads, data_axis)
-        return tuple(jnp.stack([reduced[layer_idx][which_grad] for layer_idx in range(num_layers)]) for which_grad in range(5))
-
-    row_spec = P(data_axis, None)
+            smalls[layer_idx], operands, grad_h = layer_backward(
+                grad_h, saved_acts[layer_idx], norm_gain[layer_idx], w_up[layer_idx], w_down[layer_idx], layer_idx > 0)
+            mat_operands.extend(operands)
+        gathered, small = exchange(mat_operands, jnp.concatenate(smalls), axis, chunk_cols)
+        up_full, down_full = widen(gathered, num_layers, width, hidden_width, chunk_cols)
+        small = small.reshape(num_layers, -1)
+        return (small[:, :width], up_full, small[:, width:width + hidden_width], down_full, small[:, width + hidden_width:])
+
+    row_spec = P(axis, None)
     full_spec = P()
     return jax.shard_map(
         device_grads,

time: 1760 us -> 891 us (0.51)
  waiting for transfers between devices: 1230 us -> 0 us
  Pallas kernels: 0 us -> 575 us
  matrix products: 391 us -> 276 us
  other arithmetic: 116 us -> 23.6 us
    psum x3 -> x0, waiting for transfers between devices: 1230 us -> none  [device_grads(): reduced[layer_idx] = lax.psum(local_grads, data_axis)]
    pallas_call x0 -> x3, Pallas kernels: none -> 575 us  [the longest x1 496 us: exchange(): pl.pallas_call(functools.partial(exchange_kernel, sizes), out_shape=(jax....]
    dot_general x4 -> x0, matrix products: 126 us -> none  [the longest x2 67.8 us: layer_backward(): lax.dot_general(activated, grad_b, TOKEN_DIMS, preferred_element_type=jnp...]
    another operation x4 -> x0, other arithmetic: 101 us -> none  [device_grads(): jnp.stack([reduced[layer_idx][which_grad] for layer_idx in range(num_laye...]
  transfers between devices with their start and end apart: 3 -> 0, of which waited for: 2 -> 0; matrix products, arithmetic and copies ran while one was open for 10% -> 0% of each run, Pallas kernels for 0% -> 0%
where the time goes in v2:
time: 891 us; the launch traced here: 879 us
  Pallas kernels  575 us (65%)
  matrix products  276 us (31%)
  other arithmetic  23.6 us (3%)
    pallas_call x1, Pallas kernels, exchange(): pl.pallas_call(functools.partial(exchange_kernel, sizes), out_shape=(jax....  496 us
    dot_general x2, matrix products, layer_backward(): lax.dot_general(grad_b, down_mat, FEATURE_DIMS, preferred_element_type=jn...  81.2 us
    pallas_call x2, Pallas kernels, widen(): pl.pallas_call(widen_kernel, grid=(num_layers, per_mat), in_specs=[pl.Blo...  79.3 us
    dot_general x2, matrix products, forward_stack(): jnp.dot(activated, w_down[layer_idx], preferred_element_type=jnp.float32)  74.7 us
    dot_general x2, matrix products, forward_stack(): jnp.dot(normed, w_up[layer_idx], preferred_element_type=jnp.float32)  64.5 us
    dot_general x2, matrix products, layer_backward(): lax.dot_general(grad_pre_b, up_mat, FEATURE_DIMS, preferred_element_type=...  56.1 us

profile of v2, /device:TPU:0, one launch (start us, length us, event | category | flops | bytes accessed | tf_op | source)
XLA Modules:
  0.0 879.5 jit_solution(9506248461137022746)
XLA Ops:
  0.6 2.6 fusion.62
  3.2 0.8 convert_reduce_fusion.1
  4.0 1.4 convert_reduce_fusion
  5.4 0.9 slice_convert_fusion.1
  6.3 2.7 fusion.57.refs_6_
  9.0 32.3 %fusion.9 = (bf16[1024,6144]{1,0:T(8,128)(2,1)}, bf16[1024,6144]{1,0:T(8,128)(2,1)}) fusion(f32[6144]{0:T(1024)S(1)} %bitcast.60, bf16[1024,1536]{1,0:T(8,128)(2,1)S(1)} %fusion.57.refs_6_, bf16[2,1536,6144]{2,1,0:T(8,128)(2,1)} %param.10), kind=kOutput, calls=%fused_computation.19 | convolution fusion | flops 19402850304 | bytes 47210496 | tf_op jit(solution)/shard_map/dot_general | solution.py:42
  41.4 39.9 %fusion.71 = (f32[1024]{0:T(1024)S(1)}, bf16[1024,1536]{1,0:T(8,128)(2,1)}) fusion(f32[1536]{0:T(1024)S(1)} %get-tuple-element.12, bf16[2,6144,1536]{2,1,0:T(8,128)(2,1)} %param.12, bf16[1024,6144]{1,0:T(8,128)(2,1)} %get-tuple-element.34, bf16[1024,1536]{1,0:T(8,128)(2,1)S(1)} %copy-done.6), kind=kOutput, calls=%fused_computation.85 | convolution fusion | flops 19401277440 | bytes 37758976 | tf_op jit(solution)/shard_map/dot_general | solution.py:44
  81.3 2.7 fusion.65.refs_2_
  84.0 32.2 %fusion.15 = (bf16[1024,6144]{1,0:T(8,128)(2,1)}, bf16[1024,6144]{1,0:T(8,128)(2,1)}) fusion(f32[6144]{0:T(1024)S(1)} %bitcast.59, bf16[1024,1536]{1,0:T(8,128)(2,1)S(1)} %fusion.65.refs_2_, bf16[2,1536,6144]{2,1,0:T(8,128)(2,1)} %param.10), kind=kOutput, calls=%fused_computation.25 | convolution fusion | flops 19402850304 | bytes 47210496 | tf_op jit(solution)/shard_map/dot_general | solution.py:42
  116.2 34.7 %fusion.59 = (f32[1024]{0:T(1024)S(1)}, bf16[1024,1536]{1,0:T(8,128)(2,1)}) fusion(f32[1536]{0:T(1024)S(1)} %copy-done.17, bf16[2,6144,1536]{2,1,0:T(8,128)(2,1)} %param.12, bf16[1024,6144]{1,0:T(8,128)(2,1)} %get-tuple-element.29, bf16[1024,1536]{1,0:T(8,128)(2,1)} %get-tuple-element.27), kind=kOutput, calls=%fused_computation.73 | convolution fusion | flops 19401277440 | bytes 37758976 | tf_op jit(solution)/shard_map/dot_general | solution.py:44
  151.0 3.1 fusion.60
  154.0 2.9 fusion.81.refs_1_
  157.0 40.7 %fusion.86 = (f32[6144]{0:T(1024)}, bf16[1024,6144]{1,0:T(8,128)(2,1)}) fusion(bf16[1024,6144]{1,0:T(8,128)(2,1)} %get-tuple-element.29, bf16[1024,1536]{1,0:T(8,128)(2,1)S(1)} %fusion.81.refs_1_, bf16[2,6144,1536]{2,1,0:T(8,128)(2,1)} %param.12), kind=kOutput, calls=%fused_computation.108 | convolution fusion | flops 19465758720 | bytes 47210496 | tf_op jit(solution)/shard_map/dot_general | solution.py:62
  197.7 29.3 %fusion.70 = (f32[1536]{0:T(1024)S(1)}, f32[1024]{0:T(1024)S(1)}, f32[1024,1536]{1,0:T(8,128)}) fusion(bf16[1024,1536]{1,0:T(8,128)(2,1)} %get-tuple-element.27, f32[1024]{0:T(1024)S(1)} %copy-done.13, f32[1536]{0:T(1024)S(1)} %copy-done.11, bf16[1024,6144]{1,0:T(8,128)(2,1)} %get-tuple-element.18.refs_3_, bf16[2,1536,6144]{2,1,0:T(8,128)(2,1)} %param.10), kind=kOutput, calls=%fused_computation.84 | convolution fusion | flops 19338358784 | bytes 40914944 | tf_op jit(solution)/shard_map/dot_general | solution.py:67
  227.0 6.6 fusion.84
  233.6 40.5 %fusion.87 = (f32[6144]{0:T(1024)S(1)}, bf16[1024,6144]{1,0:T(8,128)(2,1)}) fusion(bf16[1024,6144]{1,0:T(8,128)(2,1)} %get-tuple-element.34, bf16[1024,1536]{1,0:T(8,128)(2,1)S(1)} %get-tuple-element.16.refs_5_, bf16[2,6144,1536]{2,1,0:T(8,128)(2,1)} %param.12), kind=kOutput, calls=%fused_computation.109 | convolution fusion | flops 19465758720 | bytes 47210496 | tf_op jit(solution)/shard_map/dot_general | solution.py:62
  274.1 26.8 %fusion.58 = f32[1536]{0:T(1024)S(1)} fusion(bf16[1024,1536]{1,0:T(8,128)(2,1)S(1)} %copy-done.7, bf16[1024,6144]{1,0:T(8,128)(2,1)} %get-tuple-element.20.refs_7_, bf16[2,1536,6144]{2,1,0:T(8,128)(2,1)} %param.10, f32[1024]{0:T(1024)S(1)} %copy-done.16), kind=kOutput, calls=%fused_computation.72 | convolution fusion | flops 19333642240 | bytes 34613248 | tf_op jit(solution)/shard_map/dot_general | solution.py:67
  301.1 0.6 copy-done.9
  301.7 495.8 %exchange.1 = (bf16[32,2,3,256,768]{4,3,2,1,0:T(8,128)(2,1)}, f32[144,128]{1,0:T(8,128)}) custom-call(bf16[1024,6144]{1,0:T(8,128)(2,1)} %get-tuple-element.28.refs_0_, bf16[1024,1536]{1,0:T(8,128)(2,1)} %copy-done.4, bf16[1024,1536]{1,0:T(8,128)(2,1)} %copy-done.3, bf16[1024,6144]{1,0:T(8,128)(2,1)} %get-tuple-element.18.refs_3_, ...), custom_call_target="tpu_custom_call" | custom-call | tf_op jit(solution)/shard_map/exchange/pallas_call | solution.py:301
  797.5 0.9 reshape_reshape.3
  798.4 0.6 fusion.88
  799.0 0.6 slice.58
  799.7 39.7 %widen_down.1 = f32[2,6144,1536]{2,1,0:T(8,128)} custom-call(bf16[32,1536,768]{2,1,0:T(8,128)(2,1)} %bitcast.7.chunk_ref), custom_call_target="tpu_custom_call" | custom-call | tf_op jit(solution)/shard_map/widen_down/pallas_call | solution.py:355
  839.3 39.7 %widen_up.1 = f32[2,1536,6144]{2,1,0:T(8,128)} custom-call(bf16[32,1536,768]{2,1,0:T(8,128)(2,1)} %bitcast.7.chunk_ref), custom_call_target="tpu_custom_call" | custom-call | tf_op jit(solution)/shard_map/widen_up/pallas_call | solution.py:347
  (47 shorter events, 0.2 us)
Async XLA Ops:
  3.2 3.1 copy-start.15
  4.0 77.3 %copy-start.10 = (f32[1536]{0:T(1024)}, f32[1536]{0:T(1024)S(1)}, u32[]{:S(2)}) copy-start(f32[1536]{0:T(1024)S(1)} %get-tuple-element.13) | copy-start | bytes 18436
  9.0 32.4 %copy-start.2 = (bf16[1024,1536]{1,0:T(8,128)(2,1)}, bf16[1024,1536]{1,0:T(8,128)(2,1)S(1)}, u32[]{:S(2)}) copy-start(bf16[1024,1536]{1,0:T(8,128)(2,1)S(1)} %fusion.57.refs_6_) | copy-start | bytes 9437188
  9.0 32.4 %copy-start.6 = (bf16[1024,1536]{1,0:T(8,128)(2,1)S(1)}, bf16[1024,1536]{1,0:T(8,128)(2,1)}, u32[]{:S(2)}) copy-start(bf16[1024,1536]{1,0:T(8,128)(2,1)} %param.7) | copy-start | bytes 9437188
  81.3 34.9 %copy-start.12 = (f32[1024]{0:T(1024)}, f32[1024]{0:T(1024)S(1)}, u32[]{:S(2)}) copy-start(f32[1024]{0:T(1024)S(1)} %add_rsqrt_fusion.1) | copy-start | bytes 12292
  84.0 32.2 %copy-start.3 = (bf16[1024,1536]{1,0:T(8,128)(2,1)}, bf16[1024,1536]{1,0:T(8,128)(2,1)S(1)}, u32[]{:S(2)}) copy-start(bf16[1024,1536]{1,0:T(8,128)(2,1)S(1)} %fusion.65.refs_2_) | copy-start | bytes 9437188
  84.0 32.2 %copy-start.17 = (f32[1536]{0:T(1024)S(1)}, f32[1536]{0:T(1024)}, u32[]{:S(2)}) copy-start(f32[1536]{0:T(1024)} %get-tuple-element.11) | copy-start | bytes 18436
  116.2 34.8 %copy-start = (bf16[1024,1536]{1,0:T(8,128)(2,1)S(1)}, bf16[1024,1536]{1,0:T(8,128)(2,1)}, u32[]{:S(2)}) copy-start(bf16[1024,1536]{1,0:T(8,128)(2,1)} %param.8) | copy-start | bytes 9437188
  157.0 40.7 %copy-start.4 = (bf16[1024,1536]{1,0:T(8,128)(2,1)}, bf16[1024,1536]{1,0:T(8,128)(2,1)S(1)}, u32[]{:S(2)}) copy-start(bf16[1024,1536]{1,0:T(8,128)(2,1)S(1)} %fusion.81.refs_1_) | copy-start | bytes 9437188
  157.0 40.7 %copy-start.11 = (f32[1536]{0:T(1024)S(1)}, f32[1536]{0:T(1024)}, u32[]{:S(2)}) copy-start(f32[1536]{0:T(1024)} %copy-done.10) | copy-start | bytes 18436
  157.0 40.7 %copy-start.13 = (f32[1024]{0:T(1024)S(1)}, f32[1024]{0:T(1024)}, u32[]{:S(2)}) copy-start(f32[1024]{0:T(1024)} %copy-done.12) | copy-start | bytes 12292
  197.7 29.3 %copy-start.1 = (bf16[1024,1536]{1,0:T(8,128)(2,1)S(1)}, bf16[1024,1536]{1,0:T(8,128)(2,1)}, u32[]{:S(2)}) copy-start(bf16[1024,1536]{1,0:T(8,128)(2,1)} %get-tuple-element.31) | copy-start | bytes 9437188
  233.6 40.5 %copy-start.5 = (bf16[1024,1536]{1,0:T(8,128)(2,1)}, bf16[1024,1536]{1,0:T(8,128)(2,1)S(1)}, u32[]{:S(2)}) copy-start(bf16[1024,1536]{1,0:T(8,128)(2,1)S(1)} %get-tuple-element.16.refs_5_) | copy-start | bytes 9437188
  233.6 40.5 %copy-start.7 = (bf16[1024,1536]{1,0:T(8,128)(2,1)S(1)}, bf16[1024,1536]{1,0:T(8,128)(2,1)}, u32[]{:S(2)}) copy-start(bf16[1024,1536]{1,0:T(8,128)(2,1)} %param.7) | copy-start | bytes 9437188
  233.6 40.5 %copy-start.16 = (f32[1024]{0:T(1024)S(1)}, f32[1024]{0:T(1024)}, u32[]{:S(2)}) copy-start(f32[1024]{0:T(1024)} %copy-done.15) | copy-start | bytes 12292
  274.1 26.8 %copy-start.8 = (f32[18432]{0:T(1024)S(1)}, f32[18432]{0:T(1024)}, u32[]{:S(2)}) copy-start(f32[18432]{0:T(1024)} %custom-call) | copy-start | bytes 221188
  274.1 26.9 %copy-start.14 = (f32[6144]{0:T(1024)S(1)}, f32[6144]{0:T(1024)}, u32[]{:S(2)}) copy-start(f32[6144]{0:T(1024)} %get-tuple-element.17) | copy-start | bytes 73732
  301.1 0.6 copy-start.9

commit v3 on v2

--- a/solution.py
+++ b/solution.py
@@ -15,13 +15,18 @@
 CORE, DIM_X, DIM_Y, DIM_Z = range(4)
 COLOR_DIMS = ((DIM_X, DIM_Y, DIM_Z), (DIM_Y, DIM_Z, DIM_X), (DIM_Z, DIM_X, DIM_Y))
 PIPELINE = (
-    ("load", 0), ("compute_sent", 0), ("compute_kept", 0), ("send_2", 1), ("send_back_3", 2), ("send_back_core", 4),
-    ("send_1", 0), ("send_back_1", 3), ("send_3", 1), ("send_back_2", 2), ("store", 4),
+    ("load", 0), ("compute_sent", 0), ("compute_kept", 0), ("send_2", 1), ("backward_0", 0), ("send_back_3", 2), ("send_1", 0),
+    ("send_back_1", 4), ("send_back_core", 5), ("backward_1", 0), ("backward_2", 0), ("input_grad", 0), ("load_cols", 0),
+    ("send_3", 1), ("send_back_2", 2), ("store", 5),
 )
-MAX_LAG = 4
-RECV_SLOTS = 3
+MAX_LAG = 5
+RECV_SLOTS = 2
 KEPT_SLOTS = 3
 GATHER_SLOTS = 6
+TILE = 256
+NORM_ROWS = 128
+GELU_SCALE = 0.7978845608028654
+GELU_CUBIC = 0.044715
 
 
 def gelu_tanh(values):
@@ -42,8 +47,8 @@
         pre_act = (jnp.dot(normed, w_up[layer_idx], preferred_element_type=jnp.float32) + bias_up[layer_idx].astype(jnp.float32)).astype(jnp.bfloat16)
         activated = gelu_tanh(pre_act.astype(jnp.float32)).astype(jnp.bfloat16)
         branch = jnp.dot(activated, w_down[layer_idx], preferred_element_type=jnp.float32)
+        saved_acts.append((hidden, normed, pre_act, activated))
         hidden = (hid_f + branch + bias_down[layer_idx].astype(jnp.float32)).astype(jnp.bfloat16)
-        saved_acts.append((hid_scale, hid_hat, normed, pre_act, activated))
     return hidden, saved_acts
 
 
@@ -55,34 +60,24 @@
     return top_scale * (up_f - top_hat * jnp.mean(up_f * top_hat, axis=-1, keepdims=True))
 
 
-def layer_backward(grad_h, saved_layer, gain_row, up_mat, down_mat, need_input):
-    hid_scale, hid_hat, normed, pre_act, activated = saved_layer
-    grad_b = grad_h.astype(jnp.bfloat16)
-    grad_down_bias = jnp.sum(grad_h, axis=0)
-    grad_act = lax.dot_general(grad_b, down_mat, FEATURE_DIMS, preferred_element_type=jnp.float32)
-    gelu_back = jax.vjp(gelu_tanh, pre_act.astype(jnp.float32))[1]
-    grad_pre = gelu_back(grad_act)[0]
-    grad_pre_b = grad_pre.astype(jnp.bfloat16)
-    grad_up_bias = jnp.sum(grad_pre, axis=0)
-    grad_normed = lax.dot_general(grad_pre_b, up_mat, FEATURE_DIMS, preferred_element_type=jnp.float32)
-    grad_gain = jnp.sum(grad_normed * hid_hat, axis=0)
-    small = jnp.concatenate([grad_gain, grad_up_bias, grad_down_bias])
-    operands = ((activated, grad_b), (normed, grad_pre_b))
-    if not need_input:
-        return small, operands, None
-    grad_hat = grad_normed * gain_row.astype(jnp.float32)
-    grad_new = grad_h + hid_scale * (grad_hat - hid_hat * jnp.mean(grad_hat * hid_hat, axis=-1, keepdims=True))
-    return small, operands, grad_new
-
-
-def exchange_kernel(sizes, *refs):
-    num_mats, chunks_per_mat, row_dim, chunk_cols, region, down_subs, axis = sizes
-    mats = [(refs[2 * m], refs[2 * m + 1]) for m in range(num_mats)]
-    refs = refs[2 * num_mats:]
-    small_in, gathered, small_out = refs[:3]
+def gelu_slope(values):
+    square = values * values
+    bend = jnp.tanh(values * (GELU_SCALE + GELU_SCALE * GELU_CUBIC * square))
+    return 0.5 * (1.0 + bend) + (0.5 * values) * (1.0 - bend * bend) * (GELU_SCALE + 3.0 * GELU_SCALE * GELU_CUBIC * square)
+
+
+def backward_kernel(sizes, *refs):
+    num_layers, chunks_per_mat, row_dim, chunk_cols, region, down_subs, axis = sizes
+    num_mats = 2 * num_layers
+    hidden_dim = chunks_per_mat * chunk_cols
+    layer_refs = [refs[4 * n:4 * n + 4] for n in range(num_layers)]
+    refs = refs[4 * num_layers:]
+    grad_top, grad_top_b, w_up, w_down, gain_in, small_in, gathered, small_out, grad_pre_hbm, grad_b_hbm = refs[:10]
     (rows_buf, cols_buf, sent_core, kept, recv_core, sent_1, sent_2, sent_3, recv_1, recv_2, recv_3, ring,
-     small_recv, load_sem, core_send, core_recv, out_send, out_recv, back_send, back_recv, share_send, share_recv,
-     store_sem, small_send_sem, small_recv_sem) = refs[3:]
+     weight_buf, pre_buf, grad_pre_buf, grad_b, grad_normed, hid_buf, grad_buf,
+     small_recv, load_sem, grad_pre_sem, norm_sem, grad_b_sem, core_send, core_recv, out_send, out_recv, back_send, back_recv,
+     share_send, share_recv, store_sem, small_send_sem, small_recv_sem) = refs[10:]
+    small_width = 2 * row_dim + hidden_dim
     num_chunks = num_mats * chunks_per_mat
     half = COLORS * region
     me = lax.axis_index(axis)
@@ -104,29 +99,49 @@
     def rows_at(start, size):
         return pl.ds(pl.multiple_of(start, spans[2]), size)
 
-    def load_copies(mat, chunk):
+    def mat_loads(mat, chunk):
         slot = chunk % 2
         sub = chunk % chunks_per_mat
-        rows_ref, cols_ref = mats[mat]
+        layer = num_layers - 1 - mat // 2
+        _, normed, pre_act, activated = layer_refs[layer]
+        cols = pl.ds(pl.multiple_of(sub * chunk_cols, 128), chunk_cols)
         if mat % 2 == 0:
-            row_start = pl.multiple_of((sub // down_subs) * row_dim, 128)
-            col_start = pl.multiple_of((sub % down_subs) * chunk_cols, 128)
-            rows_src = rows_ref.at[:, pl.ds(row_start, row_dim)]
-            cols_src = cols_ref.at[:, pl.ds(col_start, chunk_cols)]
+            rows = pl.ds(pl.multiple_of((sub // down_subs) * row_dim, 128), row_dim)
+            return [
+                pltpu.make_async_copy(activated.at[:, rows], rows_buf.at[slot], load_sem.at[0, slot]),
+                pltpu.make_async_copy(w_down.at[layer, cols, :], weight_buf.at[slot], load_sem.at[1, slot]),
+                pltpu.make_async_copy(pre_act.at[:, cols], pre_buf.at[slot], load_sem.at[2, slot]),
+            ]
+        copies = [pltpu.make_async_copy(normed, rows_buf.at[slot], load_sem.at[0, slot])]
+        for part in range(down_subs):
+            copies.append(pltpu.make_async_copy(
+                w_up.at[layer, part * chunk_cols:(part + 1) * chunk_cols, cols],
+                weight_buf.at[slot, :, part * chunk_cols:(part + 1) * chunk_cols], load_sem.at[1 + part, slot]))
+        return copies
+
+    def cols_load(mat, chunk):
+        sub = chunk % chunks_per_mat
+        if mat % 2 == 0:
+            source = grad_top_b if mat == 0 else grad_b_hbm
+            source = source.at[:, pl.ds(pl.multiple_of((sub % down_subs) * chunk_cols, 128), chunk_cols)]
         else:
-            rows_src = rows_ref
-            cols_src = cols_ref.at[:, pl.ds(pl.multiple_of(sub * chunk_cols, 128), chunk_cols)]
-        return (
-            pltpu.make_async_copy(rows_src, rows_buf.at[slot], load_sem.at[0, slot]),
-            pltpu.make_async_copy(cols_src, cols_buf.at[slot], load_sem.at[1, slot]),
-        )
-
-    def start_loads(chunk):
+            source = grad_pre_hbm.at[sub]
+        return pltpu.make_async_copy(source, cols_buf.at[chunk % 2], load_sem.at[3, chunk % 2])
+
+    def for_mat(chunk, action):
         for mat in range(num_mats):
             @pl.when(chunk // chunks_per_mat == mat)
-            def _():
-                for copy in load_copies(mat, chunk):
-                    copy.start()
+            def _(mat=mat):
+                action(mat)
+
+    def start_loads(chunk):
+        def start(mat):
+            for copy in mat_loads(mat, chunk):
+                copy.start()
+        for_mat(chunk, start)
+
+    def grad_pre_store(sub):
+        return pltpu.make_async_copy(grad_pre_buf, grad_pre_hbm.at[sub], grad_pre_sem)
 
     def core_copy(chunk):
         slot = chunk % RECV_SLOTS
@@ -173,12 +188,26 @@
             rows_buf[slot, :, pl.ds(start, region)], cols_buf[slot], TOKEN_DIMS, preferred_element_type=jnp.float32)
 
     def load(chunk):
-        for copy in load_copies(1, chunk):
-            copy.wait()
+        def arrive(mat):
+            for copy in mat_loads(mat, chunk):
+                copy.wait()
+        for_mat(chunk, arrive)
+        for_mat(chunk, lambda mat: cols_load(mat, chunk).wait())
 
         @pl.when(chunk + 1 < num_chunks)
         def _():
             start_loads(chunk + 1)
+
+        before = chunk - 1
+
+        @pl.when((before >= 0) & ((before // chunks_per_mat) % 2 == 0))
+        def _():
+            grad_pre_store(before % chunks_per_mat).wait()
+
+    def load_cols(chunk):
+        @pl.when(chunk + 1 < num_chunks)
+        def _():
+            for_mat(chunk + 1, lambda mat: cols_load(mat, chunk + 1).start())
 
     def compute_sent(chunk):
         @pl.loop(0, COLORS)
@@ -252,19 +281,120 @@
         def _():
             store_copy(chunk - 1).wait()
 
+    token_half = grad_b.shape[0] // 2
+
+    def backward(part, chunk):
+        slot = chunk % 2
+        sub = chunk % chunks_per_mat
+        mat = chunk // chunks_per_mat
+        layer = num_layers - 1 - mat // 2
+
+        @pl.when(mat % 2 == 0)
+        def _():
+            cols = slice(part * TILE, (part + 1) * TILE)
+
+            @pl.loop(0, 2)
+            def _(which):
+                rows = pl.ds(pl.multiple_of(which * token_half, 128), token_half)
+                grad_act = lax.dot_general(
+                    grad_b[rows, :], weight_buf[slot, cols, :], FEATURE_DIMS, preferred_element_type=jnp.float32)
+                grad_pre = grad_act * gelu_slope(pre_buf[slot, rows, cols].astype(jnp.float32))
+                grad_pre_buf[rows, cols] = grad_pre.astype(jnp.bfloat16)
+                start = layer * small_width + row_dim + sub * chunk_cols + part * TILE
+                small_out[:, pl.ds(pl.multiple_of(start, 128), TILE)] += jnp.sum(grad_pre, axis=0, keepdims=True)
+
+            if part == chunk_cols // TILE - 1:
+                grad_pre_store(sub).start()
+
+        @pl.when(mat % 2 == 1)
+        def _():
+            @pl.loop(0, 2 * down_subs)
+            def _(step):
+                rows = pl.ds(pl.multiple_of((step % 2) * token_half, 128), token_half)
+                piece = part * down_subs + step // 2
+                tiles = chunk_cols // TILE
+                weight_rows = pl.ds(pl.multiple_of((piece % tiles) * TILE, TILE), TILE)
+                weight_cols = pl.ds(pl.multiple_of((piece // tiles) * chunk_cols, 128), chunk_cols)
+                out_cols = pl.ds(pl.multiple_of(piece * TILE, 128), TILE)
+                grad_normed[rows, out_cols] += lax.dot_general(
+                    cols_buf[slot, rows, :], weight_buf[slot, weight_rows, weight_cols], FEATURE_DIMS,
+                    preferred_element_type=jnp.float32)
+
+    def norm_loads(layer, block):
+        rows = pl.ds(pl.multiple_of(block * NORM_ROWS, NORM_ROWS), NORM_ROWS)
+        slot = block % 2
+        copies = [pltpu.make_async_copy(layer_refs[layer][0].at[rows, :], hid_buf.at[slot], norm_sem.at[0, slot])]
+        if layer > 0:
+            copies.append(pltpu.make_async_copy(grad_top.at[rows, :], grad_buf.at[slot], norm_sem.at[1, slot]))
+        return copies
+
+    def layer_input_grad(layer):
+        num_blocks = grad_b.shape[0] // NORM_ROWS
+        offset = layer * small_width
+        for copy in norm_loads(layer, 0):
+            copy.start()
+
+        @pl.loop(0, num_blocks)
+        def _(block):
+            @pl.when(block + 1 < num_blocks)
+            def _():
+                for copy in norm_loads(layer, block + 1):
+                    copy.start()
+            for copy in norm_loads(layer, block):
+                copy.wait()
+            rows = pl.ds(pl.multiple_of(block * NORM_ROWS, NORM_ROWS), NORM_ROWS)
+            hid_f = hid_buf[block % 2].astype(jnp.float32)
+            hid_scale = inverse_rms(hid_f)
+            hid_hat = hid_f * hid_scale
+            normed_grad = grad_normed[rows, :]
+            small_out[:, offset:offset + row_dim] += jnp.sum(normed_grad * hid_hat, axis=0, keepdims=True)
+            if layer > 0:
+                grad_normed[rows, :] = jnp.zeros((NORM_ROWS, row_dim), jnp.float32)
+                grad_hat = normed_grad * gain_in[layer:layer + 1, :]
+                grad_new = grad_buf[block % 2] + hid_scale * (
+                    grad_hat - hid_hat * jnp.mean(grad_hat * hid_hat, axis=-1, keepdims=True))
+                grad_b[rows, :] = grad_new.astype(jnp.bfloat16)
+                bias_start = offset - row_dim
+                small_out[:, bias_start:bias_start + row_dim] += jnp.sum(grad_new, axis=0, keepdims=True)
+        if layer > 0:
+            copy = pltpu.make_async_copy(grad_b, grad_b_hbm, grad_b_sem)
+            copy.start()
+            copy.wait()
+
+    def input_grad(chunk):
+        for layer in range(num_layers):
+            last = (num_layers - 1 - layer) * 2 * chunks_per_mat + 2 * chunks_per_mat - 1
+
+            @pl.when(chunk == last)
+            def _(layer=layer):
+                layer_input_grad(layer)
+
     events = dict(
         load=load, compute_sent=compute_sent, compute_kept=compute_kept, send_1=send_1, send_2=send_2, send_3=send_3,
-        send_back_3=send_back_3, send_back_2=send_back_2, send_back_1=send_back_1, send_back_core=send_back_core, store=store)
-
-    start_loads(jnp.int32(0))
+        send_back_3=send_back_3, send_back_2=send_back_2, send_back_1=send_back_1, send_back_core=send_back_core, store=store,
+        backward_0=functools.partial(backward, 0), backward_1=functools.partial(backward, 1),
+        backward_2=functools.partial(backward, 2), input_grad=input_grad, load_cols=load_cols)
+
+    first = jnp.int32(0)
+    for copy in mat_loads(0, first):
+        copy.start()
+    cols_load(0, first).start()
+    grad_b_copy = pltpu.make_async_copy(grad_top_b, grad_b, grad_b_sem)
+    grad_b_copy.start()
     barrier = pltpu.get_barrier_semaphore()
     for partner in partners:
         pl.semaphore_signal(barrier, inc=1, device_id=(partner,), device_id_type=MESH)
     small_out[...] = small_in[...]
+    grad_normed[...] = jnp.zeros_like(grad_normed)
+    grad_b_copy.wait()
     pl.semaphore_wait(barrier, 4)
 
     @pl.loop(0, num_chunks + MAX_LAG)
     def _(it):
+        for step in range(4):
+            @pl.when(it == num_chunks + step)
+            def _(step=step):
+                small_copy(step).start()
         for name, lag in PIPELINE:
             chunk = it - lag
 
@@ -272,11 +402,7 @@
             def _(name=name, chunk=chunk):
                 events[name](chunk)
         for step in range(4):
-            @pl.when(it == 2 * step + 1)
-            def _(step=step):
-                small_copy(step).start()
-
-            @pl.when(it == 2 * step + 2)
+            @pl.when(it == num_chunks + step)
             def _(step=step):
                 small_copy(step).wait()
                 small_out[...] += small_recv[step]
@@ -284,28 +410,31 @@
     store_copy(jnp.int32(num_chunks - 1)).wait()
 
 
-def exchange(mat_operands, small, axis, chunk_cols):
-    tokens, row_dim = mat_operands[1][0].shape
-    hidden = mat_operands[0][0].shape[1]
-    num_mats = len(mat_operands)
+def backward_pass(saved_acts, grad_top, norm_gain, w_up, w_down, axis, chunk_cols):
+    num_layers, row_dim, hidden = w_up.shape
+    tokens = grad_top.shape[0]
     chunks_per_mat = hidden // chunk_cols
     region = row_dim // (2 * COLORS)
     half = (COLORS, region, chunk_cols)
-    sizes = (num_mats, chunks_per_mat, row_dim, chunk_cols, region, row_dim // chunk_cols, axis)
-    num_chunks = num_mats * chunks_per_mat
-    small_rows = small.shape[0] // 128
+    sizes = (num_layers, chunks_per_mat, row_dim, chunk_cols, region, row_dim // chunk_cols, axis)
+    num_chunks = 2 * num_layers * chunks_per_mat
     bf16, f32 = jnp.bfloat16, jnp.float32
+    small_width = 2 * row_dim + hidden
+    small = jnp.zeros((1, num_layers * small_width - row_dim), f32)
+    small = jnp.concatenate([small, jnp.sum(grad_top, axis=0, keepdims=True)], axis=1)
     dma = pltpu.SemaphoreType.DMA
     any_spec = pl.BlockSpec(memory_space=pl.ANY)
     vmem_spec = pl.BlockSpec(memory_space=pltpu.VMEM)
-    gathered, small_sum = pl.pallas_call(
-        functools.partial(exchange_kernel, sizes),
+    gathered, small_sum, _, _ = pl.pallas_call(
+        functools.partial(backward_kernel, sizes),
         out_shape=(
             jax.ShapeDtypeStruct((num_chunks, 2) + half, bf16),
-            jax.ShapeDtypeStruct((small_rows, 128), f32),
+            jax.ShapeDtypeStruct(small.shape, f32),
+            jax.ShapeDtypeStruct((chunks_per_mat, tokens, chunk_cols), bf16),
+            jax.ShapeDtypeStruct((tokens, row_dim), bf16),
         ),
-        in_specs=[any_spec] * (2 * num_mats) + [vmem_spec],
-        out_specs=(any_spec, vmem_spec),
+        in_specs=[any_spec] * (4 * num_layers + 4) + [vmem_spec] * 2,
+        out_specs=(any_spec, vmem_spec, any_spec, any_spec),
         scratch_shapes=[
             pltpu.VMEM((2, tokens, row_dim), bf16),
             pltpu.VMEM((2, tokens, chunk_cols), bf16),
@@ -319,15 +448,24 @@
             pltpu.VMEM((RECV_SLOTS, COLORS, region // 4, chunk_cols), bf16),
             pltpu.VMEM((RECV_SLOTS, COLORS, region // 8, chunk_cols), bf16),
             pltpu.VMEM((GATHER_SLOTS, 2) + half, bf16),
-            pltpu.VMEM((4, small_rows, 128), f32),
-            dma((2, 2)), dma, dma((RECV_SLOTS,)), dma((3, COLORS)), dma((3, COLORS, RECV_SLOTS)),
+            pltpu.VMEM((2, chunk_cols, row_dim), bf16),
+            pltpu.VMEM((2, tokens, chunk_cols), bf16),
+            pltpu.VMEM((tokens, chunk_cols), bf16),
+            pltpu.VMEM((tokens, row_dim), bf16),
+            pltpu.VMEM((tokens, row_dim), f32),
+            pltpu.VMEM((2, NORM_ROWS, row_dim), bf16),
+            pltpu.VMEM((2, NORM_ROWS, row_dim), f32),
+            pltpu.VMEM((4,) + small.shape, f32),
+            dma((4, 2)), dma, dma((2, 2)), dma,
+            dma, dma((RECV_SLOTS,)), dma((3, COLORS)), dma((3, COLORS, RECV_SLOTS)),
             dma((3, COLORS, GATHER_SLOTS)), dma((3, COLORS, GATHER_SLOTS)), dma((GATHER_SLOTS,)), dma((GATHER_SLOTS,)),
             dma((GATHER_SLOTS,)), dma((4,)), dma((4,)),
         ],
-        compiler_params=pltpu.CompilerParams(collective_id=0, has_side_effects=True, vmem_limit_bytes=60 * 2**20),
-        name="exchange",
-    )(*[operand for pair in mat_operands for operand in pair], small.reshape(small_rows, 128))
-    return gathered, small_sum.reshape(-1)
+        compiler_params=pltpu.CompilerParams(collective_id=0, has_side_effects=True, vmem_limit_bytes=67043328),
+        name="backward",
+    )(*[array for layer in saved_acts for array in layer], grad_top, grad_top.astype(bf16), w_up, w_down,
+      norm_gain.astype(f32), small)
+    return gathered, small_sum.reshape(num_layers, small_width)
 
 
 def widen_kernel(chunk_ref, out_ref):
@@ -372,14 +510,8 @@
         chunk_cols = width // 2
         top_hidden, saved_acts = forward_stack(tokens, norm_gain, w_up, bias_up, w_down, bias_down)
         grad_h = top_gradient(top_hidden, upstream)
-        smalls, mat_operands = [None] * num_layers, []
-        for layer_idx in reversed(range(num_layers)):
-            smalls[layer_idx], operands, grad_h = layer_backward(
-                grad_h, saved_acts[layer_idx], norm_gain[layer_idx], w_up[layer_idx], w_down[layer_idx], layer_idx > 0)
-            mat_operands.extend(operands)
-        gathered, small = exchange(mat_operands, jnp.concatenate(smalls), axis, chunk_cols)
+        gathered, small = backward_pass(saved_acts, grad_h, norm_gain, w_up, w_down, axis, chunk_cols)
         up_full, down_full = widen(gathered, num_layers, width, hidden_width, chunk_cols)
-        small = small.reshape(num_layers, -1)
         return (small[:, :width], up_full, small[:, width:width + hidden_width], down_full, small[:, width + hidden_width:])
 
     row_spec = P(axis, None)

time: 891 us -> 768 us (0.86)
  matrix products: 276 us -> 139 us
  Pallas kernels: 575 us -> 589 us
    dot_general x4 -> x0, matrix products: 137 us -> none  [the longest x2 81.2 us: layer_backward(): lax.dot_general(grad_b, down_mat, FEATURE_DIMS, preferred_element_type=jn...]
    pallas_call x1, Pallas kernels: 496 us -> 509 us  [backward_pass(): pl.pallas_call(functools.partial(backward_kernel, sizes), out_shape=(jax....]
where the time goes in v3:
time: 768 us; the launch traced here: 755 us
  Pallas kernels  589 us (77%)
  matrix products  139 us (18%)
  other arithmetic  22.2 us (3%)
    pallas_call x1, Pallas kernels, backward_pass(): pl.pallas_call(functools.partial(backward_kernel, sizes), out_shape=(jax....  509 us
    pallas_call x2, Pallas kernels, widen(): pl.pallas_call(widen_kernel, grid=(num_layers, per_mat), in_specs=[pl.Blo...  79.3 us
    dot_general x2, matrix products, forward_stack(): jnp.dot(activated, w_down[layer_idx], preferred_element_type=jnp.float32)  74.5 us
    dot_general x2, matrix products, forward_stack(): jnp.dot(normed, w_up[layer_idx], preferred_element_type=jnp.float32)  64.5 us

profile of v3, /device:TPU:0, one launch (start us, length us, event | category | flops | bytes accessed | tf_op | source)
XLA Modules:
  0.0 755.2 jit_solution(11498707287527313333)
XLA Ops:
  0.6 2.6 fusion.32
  3.2 1.3 convert_element_type.75.refs_12_
  4.5 1.4 convert_reduce_fusion
  5.9 0.8 convert_reduce_fusion.1
  6.7 0.9 slice_convert_fusion
  7.6 2.7 fusion.34.refs_1_
  10.3 0.0 copy-start.1
  10.3 32.3 %fusion.5 = (bf16[1024,6144]{1,0:T(8,128)(2,1)}, bf16[1024,6144]{1,0:T(8,128)(2,1)}) fusion(f32[6144]{0:T(1024)S(1)} %bitcast.34, bf16[1024,1536]{1,0:T(8,128)(2,1)S(1)} %fusion.34.refs_1_, bf16[2,1536,6144]{2,1,0:T(8,128)(2,1)} %refs_10_.1), kind=kOutput, calls=%fused_computation.13 | convolution fusion | flops 19402850304 | bytes 47210496 | tf_op jit(solution)/shard_map/dot_general | solution.py:47
  42.6 39.8 %fusion.37 = (f32[1024]{0:T(1024)S(1)}, bf16[1024,1536]{1,0:T(8,128)(2,1)}) fusion(f32[1536]{0:T(1024)S(1)} %get-tuple-element.10, bf16[2,6144,1536]{2,1,0:T(8,128)(2,1)} %refs_11_.1, bf16[1024,6144]{1,0:T(8,128)(2,1)} %get-tuple-element.20.refs_2_, bf16[1024,1536]{1,0:T(8,128)(2,1)S(1)} %copy-done.1), kind=kOutput, calls=%fused_computation.53 | convolution fusion | flops 19401277440 | bytes 37758976 | tf_op jit(solution)/shard_map/dot_general | solution.py:49
  82.5 2.7 fusion.39.refs_5_
  85.2 32.2 %fusion.11 = (bf16[1024,6144]{1,0:T(8,128)(2,1)}, bf16[1024,6144]{1,0:T(8,128)(2,1)}) fusion(f32[6144]{0:T(1024)S(1)} %bitcast.33, bf16[1024,1536]{1,0:T(8,128)(2,1)S(1)} %fusion.39.refs_5_, bf16[2,1536,6144]{2,1,0:T(8,128)(2,1)} %refs_10_.1), kind=kOutput, calls=%fused_computation.19 | convolution fusion | flops 19402850304 | bytes 47210496 | tf_op jit(solution)/shard_map/dot_general | solution.py:47
  117.3 34.7 %fusion.29 = (f32[1024]{0:T(1024)S(1)}, bf16[1024,1536]{1,0:T(8,128)(2,1)}) fusion(f32[1536]{0:T(1024)S(1)} %copy-done.5, bf16[2,6144,1536]{2,1,0:T(8,128)(2,1)} %refs_11_.1, bf16[1024,6144]{1,0:T(8,128)(2,1)} %get-tuple-element.24.refs_6_, bf16[1024,1536]{1,0:T(8,128)(2,1)} %get-tuple-element.22.refs_4_), kind=kOutput, calls=%fused_computation.45 | convolution fusion | flops 19401277440 | bytes 37758976 | tf_op jit(solution)/shard_map/dot_general | solution.py:49
  152.0 3.1 fusion.30
  155.1 3.1 fusion.48
  158.2 0.8 concatenate.3.refs_13_
  159.0 1.8 copy-done
  160.8 2.1 convert_element_type.74.refs_9_
  162.9 509.3 %backward.1 = (bf16[32,2,3,256,768]{4,3,2,1,0:T(8,128)(2,1)}, f32[1,18432]{1,0:T(1,128)}, bf16[8,1024,768]{2,1,0:T(8,128)(2,1)}, bf16[1024,1536]{1,0:T(8,128)(2,1)}) custom-call(bf16[1024,1536]{1,0:T(8,128)(2,1)} %refs_0_.1, bf16[1024,1536]{1,0:T(8,128)(2,1)} %copy-done.3, bf16[1024,6144]{1,0:T(8,128)(2,1)} %get-tuple-element.20.refs_2_, ...), custom_call_target="tpu_custom_call" | custom-call | tf_op jit(solution)/shard_map/backward/pallas_call | solution.py:428
  672.2 0.5 broadcast.95
  672.7 1.7 reduce.11
  674.5 0.6 fusion.50
  675.1 0.6 slice.53
  675.7 39.7 %widen_down.1 = f32[2,6144,1536]{2,1,0:T(8,128)} custom-call(bf16[32,1536,768]{2,1,0:T(8,128)(2,1)} %bitcast.6.chunk_ref), custom_call_target="tpu_custom_call" | custom-call | tf_op jit(solution)/shard_map/widen_down/pallas_call | solution.py:493
  715.4 39.7 %widen_up.1 = f32[2,1536,6144]{2,1,0:T(8,128)} custom-call(bf16[32,1536,768]{2,1,0:T(8,128)(2,1)} %bitcast.6.chunk_ref), custom_call_target="tpu_custom_call" | custom-call | tf_op jit(solution)/shard_map/widen_up/pallas_call | solution.py:485
  (16 shorter events, 0.1 us)
Async XLA Ops:
  10.3 32.4 %copy-start.3 = (bf16[1024,1536]{1,0:T(8,128)(2,1)}, bf16[1024,1536]{1,0:T(8,128)(2,1)S(1)}, u32[]{:S(2)}) copy-start(bf16[1024,1536]{1,0:T(8,128)(2,1)S(1)} %fusion.34.refs_1_) | copy-start | bytes 9437188
  10.3 32.4 %copy-start.1 = (bf16[1024,1536]{1,0:T(8,128)(2,1)S(1)}, bf16[1024,1536]{1,0:T(8,128)(2,1)}, u32[]{:S(2)}) copy-start(bf16[1024,1536]{1,0:T(8,128)(2,1)} %refs_0_.1) | copy-start | bytes 9437188
  85.1 32.2 %copy-start.4 = (bf16[1024,1536]{1,0:T(8,128)(2,1)}, bf16[1024,1536]{1,0:T(8,128)(2,1)S(1)}, u32[]{:S(2)}) copy-start(bf16[1024,1536]{1,0:T(8,128)(2,1)S(1)} %fusion.39.refs_5_) | copy-start | bytes 9437188
  85.1 32.2 %copy-start.5 = (f32[1536]{0:T(1024)S(1)}, f32[1536]{0:T(1024)}, u32[]{:S(2)}) copy-start(f32[1536]{0:T(1024)} %get-tuple-element.9) | copy-start | bytes 18436
  117.3 34.7 %copy-start.2 = (bf16[1024,1536]{1,0:T(8,128)(2,1)S(1)}, bf16[1024,1536]{1,0:T(8,128)(2,1)}, u32[]{:S(2)}) copy-start(bf16[1024,1536]{1,0:T(8,128)(2,1)} %param.8) | copy-start | bytes 9437188
  158.2 2.6 copy-start

commit v4 on v3

--- a/solution.py
+++ b/solution.py
@@ -29,35 +29,218 @@
 GELU_CUBIC = 0.044715
 
 
-def gelu_tanh(values):
-    return jax.nn.gelu(values, approximate=True)
-
-
 def inverse_rms(hid_f):
     return lax.rsqrt(jnp.mean(hid_f * hid_f, axis=-1, keepdims=True) + EPSILON)
 
 
-def forward_stack(hidden, norm_gain, w_up, bias_up, w_down, bias_down):
-    saved_acts = []
-    for layer_idx in range(norm_gain.shape[0]):
-        hid_f = hidden.astype(jnp.float32)
-        hid_scale = inverse_rms(hid_f)
-        hid_hat = hid_f * hid_scale
-        normed = (hid_hat * norm_gain[layer_idx].astype(jnp.float32)).astype(jnp.bfloat16)
-        pre_act = (jnp.dot(normed, w_up[layer_idx], preferred_element_type=jnp.float32) + bias_up[layer_idx].astype(jnp.float32)).astype(jnp.bfloat16)
-        activated = gelu_tanh(pre_act.astype(jnp.float32)).astype(jnp.bfloat16)
-        branch = jnp.dot(activated, w_down[layer_idx], preferred_element_type=jnp.float32)
-        saved_acts.append((hidden, normed, pre_act, activated))
-        hidden = (hid_f + branch + bias_down[layer_idx].astype(jnp.float32)).astype(jnp.bfloat16)
-    return hidden, saved_acts
-
-
-def top_gradient(top_hidden, upstream):
-    top_f = top_hidden.astype(jnp.float32)
-    top_scale = inverse_rms(top_f)
-    top_hat = top_f * top_scale
-    up_f = upstream.astype(jnp.float32)
-    return top_scale * (up_f - top_hat * jnp.mean(up_f * top_hat, axis=-1, keepdims=True))
+def gelu(values):
+    return (0.5 * values) * (1.0 + jnp.tanh(values * (GELU_SCALE + GELU_SCALE * GELU_CUBIC * (values * values))))
+
+
+def forward_kernel(
+    sizes, tokens, upstream, w_up, w_down, gain_in, bias_up, bias_down, hid_out, normed_out, pre_act_out, act_out,
+    grad_top_out, grad_top_b_out, small_out, hid, normed, branch, up_buf, down_buf, pre_buf, act_buf, up_rows, grad_b_buf,
+    io_sem, up_sem, down_sem, pre_sem, act_sem,
+):
+    num_layers, num_tiles, tile_cols = sizes
+    num_tokens, row_dim = hid.shape
+    steps = num_tiles + 1
+    token_half = num_tokens // 2
+    parts = tile_cols // TILE
+    branch_cols = row_dim // parts
+
+    def up_load(step):
+        layer, tile = step // steps, step % steps
+        cols = pl.ds(pl.multiple_of(tile * tile_cols, 128), tile_cols)
+        return pltpu.make_async_copy(w_up.at[layer, :, cols], up_buf.at[tile % 2], up_sem.at[tile % 2])
+
+    def down_load(step):
+        layer, tile = step // steps, step % steps
+        rows = pl.ds(pl.multiple_of(tile * tile_cols, 128), tile_cols)
+        return pltpu.make_async_copy(w_down.at[layer, rows, :], down_buf.at[tile % 2], down_sem.at[tile % 2])
+
+    def tile_stores(step):
+        layer, tile = step // steps, step % steps
+        cols = pl.ds(pl.multiple_of(tile * tile_cols, 128), tile_cols)
+        return (
+            pltpu.make_async_copy(pre_buf.at[tile % 2], pre_act_out.at[layer, :, cols], pre_sem.at[tile % 2]),
+            pltpu.make_async_copy(act_buf.at[tile % 2], act_out.at[layer, :, cols], act_sem.at[tile % 2]),
+        )
+
+    def normed_store(layer):
+        return pltpu.make_async_copy(normed, normed_out.at[layer], io_sem.at[1])
+
+    def hid_store():
+        return pltpu.make_async_copy(hid, hid_out, io_sem.at[2])
+
+    tokens_load = pltpu.make_async_copy(tokens, hid, io_sem.at[0])
+    tokens_load.start()
+    first = jnp.int32(0)
+    up_load(first).start()
+    down_load(first).start()
+    upstream_load = pltpu.make_async_copy(upstream, up_rows, io_sem.at[3])
+    upstream_load.start()
+    tokens_load.wait()
+
+    def norm_rows(layer):
+        @pl.loop(0, num_tokens // NORM_ROWS)
+        def _(block):
+            rows = pl.ds(pl.multiple_of(block * NORM_ROWS, NORM_ROWS), NORM_ROWS)
+            hid_f = hid[rows, :].astype(jnp.float32)
+            gain = gain_in[pl.ds(layer, 1), :]
+            normed[rows, :] = ((hid_f * inverse_rms(hid_f)) * gain).astype(jnp.bfloat16)
+
+    def add_branch(layer):
+        @pl.loop(0, num_tokens // NORM_ROWS)
+        def _(block):
+            rows = pl.ds(pl.multiple_of(block * NORM_ROWS, NORM_ROWS), NORM_ROWS)
+            bias = bias_down[pl.ds(layer, 1), :]
+            hid[rows, :] = ((hid[rows, :].astype(jnp.float32) + branch[rows, :]) + bias).astype(jnp.bfloat16)
+
+    def work(step, with_up, with_down):
+        layer, tile = step // steps, step % steps
+
+        @pl.loop(0, 2 * parts)
+        def _(index):
+            rows = pl.ds(pl.multiple_of((index % 2) * token_half, 128), token_half)
+            part = index // 2
+            if with_up:
+                cols = pl.ds(pl.multiple_of(part * TILE, TILE), TILE)
+                bias = bias_up[pl.ds(layer, 1), pl.ds(pl.multiple_of(tile * tile_cols + part * TILE, TILE), TILE)]
+                pre_act = (jnp.dot(normed[rows, :], up_buf[tile % 2, :, cols], preferred_element_type=jnp.float32) + bias).astype(jnp.bfloat16)
+                pre_buf[tile % 2, rows, cols] = pre_act
+                act_buf[tile % 2, rows, cols] = gelu(pre_act.astype(jnp.float32)).astype(jnp.bfloat16)
+            if with_down:
+                cols = pl.ds(pl.multiple_of(part * branch_cols, 128), branch_cols)
+                last = (tile + 1) % 2
+                added = jnp.dot(act_buf[last, rows, :], down_buf[last, :, cols], preferred_element_type=jnp.float32)
+                branch[rows, cols] += added
+
+    branch[...] = jnp.zeros_like(branch)
+
+    @pl.loop(0, num_layers * steps)
+    def _(step):
+        layer, tile = step // steps, step % steps
+
+        @pl.when(tile < num_tiles)
+        def _():
+            up_load(step).wait()
+
+            @pl.when(tile + 1 < num_tiles)
+            def _():
+                up_load(step + 1).start()
+
+        @pl.when(tile > 0)
+        def _():
+            down_load(step - 1).wait()
+
+            @pl.when(tile < num_tiles)
+            def _():
+                down_load(step).start()
+
+        @pl.when((tile == num_tiles) & (layer + 1 < num_layers))
+        def _():
+            up_load(step + 1).start()
+            down_load(step + 1).start()
+
+        @pl.when((tile > 1) & (tile < num_tiles))
+        def _():
+            for copy in tile_stores(step - 2):
+                copy.wait()
+
+        @pl.when(tile == 0)
+        def _():
+            @pl.when(layer > 0)
+            def _():
+                normed_store(layer - 1).wait()
+            norm_rows(layer)
+            normed_store(layer).start()
+            work(step, True, False)
+
+        @pl.when((tile > 0) & (tile < num_tiles))
+        def _():
+            work(step, True, True)
+
+        @pl.when(tile < num_tiles)
+        def _():
+            for copy in tile_stores(step):
+                copy.start()
+
+        @pl.when(tile == num_tiles)
+        def _():
+            work(step, False, True)
+            for back in (2, 1):
+                for copy in tile_stores(step - back):
+                    copy.wait()
+            add_branch(layer)
+
+            @pl.when(layer + 1 < num_layers)
+            def _():
+                hid_store().start()
+                branch[...] = jnp.zeros_like(branch)
+                hid_store().wait()
+
+    normed_store(num_layers - 1).wait()
+    upstream_load.wait()
+    small_out[...] = jnp.zeros_like(small_out)
+    bias_start = small_out.shape[1] - row_dim
+
+    @pl.loop(0, num_tokens // NORM_ROWS)
+    def _(block):
+        rows = pl.ds(pl.multiple_of(block * NORM_ROWS, NORM_ROWS), NORM_ROWS)
+        top_f = hid[rows, :].astype(jnp.float32)
+        top_scale = inverse_rms(top_f)
+        top_hat = top_f * top_scale
+        up_f = up_rows[rows, :].astype(jnp.float32)
+        grad = top_scale * (up_f - top_hat * jnp.mean(up_f * top_hat, axis=-1, keepdims=True))
+        branch[rows, :] = grad
+        grad_b_buf[rows, :] = grad.astype(jnp.bfloat16)
+        small_out[:, bias_start:bias_start + row_dim] += jnp.sum(grad, axis=0, keepdims=True)
+    grad_store = pltpu.make_async_copy(branch, grad_top_out, io_sem.at[0])
+    grad_b_store = pltpu.make_async_copy(grad_b_buf, grad_top_b_out, io_sem.at[1])
+    grad_store.start()
+    grad_b_store.start()
+    grad_store.wait()
+    grad_b_store.wait()
+
+
+def forward_pass(tokens, upstream, norm_gain, w_up, bias_up, w_down, bias_down, tile_cols):
+    num_tokens, row_dim = tokens.shape
+    num_layers, _, hidden = w_up.shape
+    bf16, f32 = jnp.bfloat16, jnp.float32
+    dma = pltpu.SemaphoreType.DMA
+    any_spec = pl.BlockSpec(memory_space=pl.ANY)
+    vmem_spec = pl.BlockSpec(memory_space=pltpu.VMEM)
+    rows = (num_tokens, row_dim)
+    wide = (num_layers, num_tokens, hidden)
+    return pl.pallas_call(
+        functools.partial(forward_kernel, (num_layers, hidden // tile_cols, tile_cols)),
+        out_shape=(
+            jax.ShapeDtypeStruct(rows, bf16),
+            jax.ShapeDtypeStruct((num_layers,) + rows, bf16),
+            jax.ShapeDtypeStruct(wide, bf16),
+            jax.ShapeDtypeStruct(wide, bf16),
+            jax.ShapeDtypeStruct(rows, f32),
+            jax.ShapeDtypeStruct(rows, bf16),
+            jax.ShapeDtypeStruct((1, num_layers * (2 * row_dim + hidden)), f32),
+        ),
+        in_specs=[any_spec] * 4 + [vmem_spec] * 3,
+        out_specs=(any_spec,) * 6 + (vmem_spec,),
+        scratch_shapes=[
+            pltpu.VMEM(rows, bf16),
+            pltpu.VMEM(rows, bf16),
+            pltpu.VMEM(rows, f32),
+            pltpu.VMEM((2, row_dim, tile_cols), bf16),
+            pltpu.VMEM((2, tile_cols, row_dim), bf16),
+            pltpu.VMEM((2, num_tokens, tile_cols), bf16),
+            pltpu.VMEM((2, num_tokens, tile_cols), bf16),
+            pltpu.VMEM(rows, bf16),
+            pltpu.VMEM(rows, bf16),
+            dma((4,)), dma((2,)), dma((2,)), dma((2,)), dma((2,)),
+        ],
+        compiler_params=pltpu.CompilerParams(vmem_limit_bytes=60 * 2**20),
+        name="forward",
+    )(tokens, upstream, w_up, w_down, norm_gain.astype(f32), bias_up.astype(f32), bias_down.astype(f32))
 
 
 def gelu_slope(values):
@@ -70,13 +253,13 @@
     num_layers, chunks_per_mat, row_dim, chunk_cols, region, down_subs, axis = sizes
     num_mats = 2 * num_layers
     hidden_dim = chunks_per_mat * chunk_cols
-    layer_refs = [refs[4 * n:4 * n + 4] for n in range(num_layers)]
-    refs = refs[4 * num_layers:]
-    grad_top, grad_top_b, w_up, w_down, gain_in, small_in, gathered, small_out, grad_pre_hbm, grad_b_hbm = refs[:10]
+    hid_refs, refs = refs[:num_layers], refs[num_layers:]
+    (normed, pre_act, activated, grad_top, grad_top_b, w_up, w_down, gain_in, small_in,
+     gathered, small_out, grad_pre_hbm, grad_b_hbm) = refs[:13]
     (rows_buf, cols_buf, sent_core, kept, recv_core, sent_1, sent_2, sent_3, recv_1, recv_2, recv_3, ring,
      weight_buf, pre_buf, grad_pre_buf, grad_b, grad_normed, hid_buf, grad_buf,
      small_recv, load_sem, grad_pre_sem, norm_sem, grad_b_sem, core_send, core_recv, out_send, out_recv, back_send, back_recv,
-     share_send, share_recv, store_sem, small_send_sem, small_recv_sem) = refs[10:]
+     share_send, share_recv, store_sem, small_send_sem, small_recv_sem) = refs[13:]
     small_width = 2 * row_dim + hidden_dim
     num_chunks = num_mats * chunks_per_mat
     half = COLORS * region
@@ -103,16 +286,15 @@
         slot = chunk % 2
         sub = chunk % chunks_per_mat
         layer = num_layers - 1 - mat // 2
-        _, normed, pre_act, activated = layer_refs[layer]
         cols = pl.ds(pl.multiple_of(sub * chunk_cols, 128), chunk_cols)
         if mat % 2 == 0:
             rows = pl.ds(pl.multiple_of((sub // down_subs) * row_dim, 128), row_dim)
             return [
-                pltpu.make_async_copy(activated.at[:, rows], rows_buf.at[slot], load_sem.at[0, slot]),
+                pltpu.make_async_copy(activated.at[layer, :, rows], rows_buf.at[slot], load_sem.at[0, slot]),
                 pltpu.make_async_copy(w_down.at[layer, cols, :], weight_buf.at[slot], load_sem.at[1, slot]),
-                pltpu.make_async_copy(pre_act.at[:, cols], pre_buf.at[slot], load_sem.at[2, slot]),
+                pltpu.make_async_copy(pre_act.at[layer, :, cols], pre_buf.at[slot], load_sem.at[2, slot]),
             ]
-        copies = [pltpu.make_async_copy(normed, rows_buf.at[slot], load_sem.at[0, slot])]
+        copies = [pltpu.make_async_copy(normed.at[layer], rows_buf.at[slot], load_sem.at[0, slot])]
         for part in range(down_subs):
             copies.append(pltpu.make_async_copy(
                 w_up.at[layer, part * chunk_cols:(part + 1) * chunk_cols, cols],
@@ -323,7 +505,7 @@
     def norm_loads(layer, block):
         rows = pl.ds(pl.multiple_of(block * NORM_ROWS, NORM_ROWS), NORM_ROWS)
         slot = block % 2
-        copies = [pltpu.make_async_copy(layer_refs[layer][0].at[rows, :], hid_buf.at[slot], norm_sem.at[0, slot])]
+        copies = [pltpu.make_async_copy(hid_refs[layer].at[rows, :], hid_buf.at[slot], norm_sem.at[0, slot])]
         if layer > 0:
             copies.append(pltpu.make_async_copy(grad_top.at[rows, :], grad_buf.at[slot], norm_sem.at[1, slot]))
         return copies
@@ -410,7 +592,7 @@
     store_copy(jnp.int32(num_chunks - 1)).wait()
 
 
-def backward_pass(saved_acts, grad_top, norm_gain, w_up, w_down, axis, chunk_cols):
+def backward_pass(hid_rows, saved, grad_top, grad_top_b, norm_gain, w_up, w_down, small, axis, chunk_cols):
     num_layers, row_dim, hidden = w_up.shape
     tokens = grad_top.shape[0]
     chunks_per_mat = hidden // chunk_cols
@@ -420,8 +602,6 @@
     num_chunks = 2 * num_layers * chunks_per_mat
     bf16, f32 = jnp.bfloat16, jnp.float32
     small_width = 2 * row_dim + hidden
-    small = jnp.zeros((1, num_layers * small_width - row_dim), f32)
-    small = jnp.concatenate([small, jnp.sum(grad_top, axis=0, keepdims=True)], axis=1)
     dma = pltpu.SemaphoreType.DMA
     any_spec = pl.BlockSpec(memory_space=pl.ANY)
     vmem_spec = pl.BlockSpec(memory_space=pltpu.VMEM)
@@ -433,7 +613,7 @@
             jax.ShapeDtypeStruct((chunks_per_mat, tokens, chunk_cols), bf16),
             jax.ShapeDtypeStruct((tokens, row_dim), bf16),
         ),
-        in_specs=[any_spec] * (4 * num_layers + 4) + [vmem_spec] * 2,
+        in_specs=[any_spec] * (num_layers + 7) + [vmem_spec] * 2,
         out_specs=(any_spec, vmem_spec, any_spec, any_spec),
         scratch_shapes=[
             pltpu.VMEM((2, tokens, row_dim), bf16),
@@ -463,8 +643,7 @@
         ],
         compiler_params=pltpu.CompilerParams(collective_id=0, has_side_effects=True, vmem_limit_bytes=67043328),
         name="backward",
-    )(*[array for layer in saved_acts for array in layer], grad_top, grad_top.astype(bf16), w_up, w_down,
-      norm_gain.astype(f32), small)
+    )(*hid_rows, *saved, grad_top, grad_top_b, w_up, w_down, norm_gain.astype(f32), small)
     return gathered, small_sum.reshape(num_layers, small_width)
 
 
@@ -508,9 +687,10 @@
         num_layers, width = norm_gain.shape
         hidden_width = w_up.shape[2]
         chunk_cols = width // 2
-        top_hidden, saved_acts = forward_stack(tokens, norm_gain, w_up, bias_up, w_down, bias_down)
-        grad_h = top_gradient(top_hidden, upstream)
-        gathered, small = backward_pass(saved_acts, grad_h, norm_gain, w_up, w_down, axis, chunk_cols)
+        hid_1, normed, pre_act, activated, grad_top, grad_top_b, small = forward_pass(
+            tokens, upstream, norm_gain, w_up, bias_up, w_down, bias_down, chunk_cols)
+        gathered, small = backward_pass(
+            (tokens, hid_1), (normed, pre_act, activated), grad_top, grad_top_b, norm_gain, w_up, w_down, small, axis, chunk_cols)
         up_full, down_full = widen(gathered, num_layers, width, hidden_width, chunk_cols)
         return (small[:, :width], up_full, small[:, width:width + hidden_width], down_full, small[:, width + hidden_width:])
 

time: 768 us -> 796 us (1.036); the launches traced: 755 us -> 795 us
  Pallas kernels: 589 us -> 787 us
  matrix products: 139 us -> 0 us
  other arithmetic: 22.2 us -> 5.67 us
    pallas_call x0 -> x1, Pallas kernels: none -> 198 us  [forward_pass(): pl.pallas_call(functools.partial(forward_kernel, (num_layers, hidden // t...]
    dot_general x4 -> x0, matrix products: 139 us -> none  [the longest x2 74.5 us: forward_stack(): jnp.dot(activated, w_down[layer_idx], preferred_element_type=jnp.float32)]
    reduce_sum x3 -> x0, other arithmetic: 8.69 us -> none  [the longest x1 3.06 us: top_gradient(): jnp.mean(up_f * top_hat, axis=-1, keepdims=True)]
where the time goes in v4:
time: 796 us; the launch traced here: 795 us
  Pallas kernels  787 us (99%)
    pallas_call x1, Pallas kernels, backward_pass(): pl.pallas_call(functools.partial(backward_kernel, sizes), out_shape=(jax....  509 us
    pallas_call x1, Pallas kernels, forward_pass(): pl.pallas_call(functools.partial(forward_kernel, (num_layers, hidden // t...  198 us
    pallas_call x2, Pallas kernels, widen(): pl.pallas_call(widen_kernel, grid=(num_layers, per_mat), in_specs=[pl.Blo...  79.3 us

profile of v4, /device:TPU:0, one launch (start us, length us, event | category | flops | bytes accessed | tf_op | source)
XLA Modules:
  0.0 794.8 jit_solution(14137004879674652001)
XLA Ops:
  0.6 1.3 convert_element_type.10.gain_in.refs_9_
  1.9 1.3 convert_element_type.12.bias_down
  3.2 1.4 convert_element_type.11.bias_up
  4.6 198.2 %forward.1 = (bf16[1024,1536]{1,0:T(8,128)(2,1)}, bf16[2,1024,1536]{2,1,0:T(8,128)(2,1)}, bf16[2,1024,6144]{2,1,0:T(8,128)(2,1)}, bf16[2,1024,6144]{2,1,0:T(8,12...) custom-call(bf16[1024,1536]{1,0:T(8,128)(2,1)} %refs_0_.1, ...), custom_call_target="tpu_custom_call" | custom-call | tf_op jit(solution)/shard_map/forward/pallas_call | solution.py:216
  202.8 509.2 %backward.1 = (bf16[32,2,3,256,768]{4,3,2,1,0:T(8,128)(2,1)}, f32[1,18432]{1,0:T(1,128)}, bf16[8,1024,768]{2,1,0:T(8,128)(2,1)}, bf16[1024,1536]{1,0:T(8,128)(2,1)}) custom-call(bf16[1024,1536]{1,0:T(8,128)(2,1)} %refs_0_.1, bf16[1024,1536]{1,0:T(8,128)(2,1)} %get-tuple-element.14.refs_1_, bf16[2,1024,1536]{2,1,0:T(8,128)(2,1)} %get-tuple-element.15.refs_2_, ...), custom_call_target="tpu_custom_call" | custom-call | tf_op jit(solution)/shard_map/backward/pallas_call | solution.py:608
  712.0 0.5 broadcast.3
  712.5 1.7 reduce.3
  714.3 0.6 fusion
  714.9 0.6 slice.13
  715.5 39.7 %widen_down.1 = f32[2,6144,1536]{2,1,0:T(8,128)} custom-call(bf16[32,1536,768]{2,1,0:T(8,128)(2,1)} %bitcast.chunk_ref), custom_call_target="tpu_custom_call" | custom-call | tf_op jit(solution)/shard_map/widen_down/pallas_call | solution.py:672
  755.2 39.7 %widen_up.1 = f32[2,1536,6144]{2,1,0:T(8,128)} custom-call(bf16[32,1536,768]{2,1,0:T(8,128)(2,1)} %bitcast.chunk_ref), custom_call_target="tpu_custom_call" | custom-call | tf_op jit(solution)/shard_map/widen_up/pallas_call | solution.py:664
  (1 shorter events, 0.0 us)

commit v5 on v4

--- a/solution.py
+++ b/solution.py
@@ -24,6 +24,7 @@
 KEPT_SLOTS = 3
 GATHER_SLOTS = 6
 TILE = 256
+UP_COLS = 512
 NORM_ROWS = 128
 GELU_SCALE = 0.7978845608028654
 GELU_CUBIC = 0.044715
@@ -44,34 +45,24 @@
 ):
     num_layers, num_tiles, tile_cols = sizes
     num_tokens, row_dim = hid.shape
-    steps = num_tiles + 1
     token_half = num_tokens // 2
-    parts = tile_cols // TILE
-    branch_cols = row_dim // parts
+    num_steps = num_layers * num_tiles
 
     def up_load(step):
-        layer, tile = step // steps, step % steps
-        cols = pl.ds(pl.multiple_of(tile * tile_cols, 128), tile_cols)
-        return pltpu.make_async_copy(w_up.at[layer, :, cols], up_buf.at[tile % 2], up_sem.at[tile % 2])
+        cols = pl.ds(pl.multiple_of((step % num_tiles) * tile_cols, 128), tile_cols)
+        return pltpu.make_async_copy(w_up.at[step // num_tiles, :, cols], up_buf.at[step % 2], up_sem.at[step % 2])
 
     def down_load(step):
-        layer, tile = step // steps, step % steps
-        rows = pl.ds(pl.multiple_of(tile * tile_cols, 128), tile_cols)
-        return pltpu.make_async_copy(w_down.at[layer, rows, :], down_buf.at[tile % 2], down_sem.at[tile % 2])
+        rows = pl.ds(pl.multiple_of((step % num_tiles) * tile_cols, 128), tile_cols)
+        return pltpu.make_async_copy(w_down.at[step // num_tiles, rows, :], down_buf.at[step % 2], down_sem.at[step % 2])
 
     def tile_stores(step):
-        layer, tile = step // steps, step % steps
-        cols = pl.ds(pl.multiple_of(tile * tile_cols, 128), tile_cols)
+        cols = pl.ds(pl.multiple_of((step % num_tiles) * tile_cols, 128), tile_cols)
+        layer, slot = step // num_tiles, step % 2
         return (
-            pltpu.make_async_copy(pre_buf.at[tile % 2], pre_act_out.at[layer, :, cols], pre_sem.at[tile % 2]),
-            pltpu.make_async_copy(act_buf.at[tile % 2], act_out.at[layer, :, cols], act_sem.at[tile % 2]),
+            pltpu.make_async_copy(pre_buf.at[slot], pre_act_out.at[layer, :, cols], pre_sem.at[slot]),
+            pltpu.make_async_copy(act_buf.at[slot], act_out.at[layer, :, cols], act_sem.at[slot]),
         )
-
-    def normed_store(layer):
-        return pltpu.make_async_copy(normed, normed_out.at[layer], io_sem.at[1])
-
-    def hid_store():
-        return pltpu.make_async_copy(hid, hid_out, io_sem.at[2])
 
     tokens_load = pltpu.make_async_copy(tokens, hid, io_sem.at[0])
     tokens_load.start()
@@ -80,115 +71,101 @@
     down_load(first).start()
     upstream_load = pltpu.make_async_copy(upstream, up_rows, io_sem.at[3])
     upstream_load.start()
+    small_out[...] = jnp.zeros_like(small_out)
     tokens_load.wait()
 
-    def norm_rows(layer):
+    def each_block(action):
         @pl.loop(0, num_tokens // NORM_ROWS)
         def _(block):
-            rows = pl.ds(pl.multiple_of(block * NORM_ROWS, NORM_ROWS), NORM_ROWS)
-            hid_f = hid[rows, :].astype(jnp.float32)
-            gain = gain_in[pl.ds(layer, 1), :]
-            normed[rows, :] = ((hid_f * inverse_rms(hid_f)) * gain).astype(jnp.bfloat16)
-
-    def add_branch(layer):
-        @pl.loop(0, num_tokens // NORM_ROWS)
-        def _(block):
-            rows = pl.ds(pl.multiple_of(block * NORM_ROWS, NORM_ROWS), NORM_ROWS)
-            bias = bias_down[pl.ds(layer, 1), :]
-            hid[rows, :] = ((hid[rows, :].astype(jnp.float32) + branch[rows, :]) + bias).astype(jnp.bfloat16)
-
-    def work(step, with_up, with_down):
-        layer, tile = step // steps, step % steps
-
-        @pl.loop(0, 2 * parts)
-        def _(index):
-            rows = pl.ds(pl.multiple_of((index % 2) * token_half, 128), token_half)
-            part = index // 2
-            if with_up:
-                cols = pl.ds(pl.multiple_of(part * TILE, TILE), TILE)
-                bias = bias_up[pl.ds(layer, 1), pl.ds(pl.multiple_of(tile * tile_cols + part * TILE, TILE), TILE)]
-                pre_act = (jnp.dot(normed[rows, :], up_buf[tile % 2, :, cols], preferred_element_type=jnp.float32) + bias).astype(jnp.bfloat16)
-                pre_buf[tile % 2, rows, cols] = pre_act
-                act_buf[tile % 2, rows, cols] = gelu(pre_act.astype(jnp.float32)).astype(jnp.bfloat16)
-            if with_down:
-                cols = pl.ds(pl.multiple_of(part * branch_cols, 128), branch_cols)
-                last = (tile + 1) % 2
-                added = jnp.dot(act_buf[last, rows, :], down_buf[last, :, cols], preferred_element_type=jnp.float32)
-                branch[rows, cols] += added
-
+            action(pl.ds(pl.multiple_of(block * NORM_ROWS, NORM_ROWS), NORM_ROWS))
+
+    def normalize(layer, rows, hid_f):
+        normed[rows, :] = ((hid_f * inverse_rms(hid_f)) * gain_in[layer:layer + 1, :]).astype(jnp.bfloat16)
+
+    def first_rows(rows):
+        normalize(0, rows, hid[rows, :].astype(jnp.float32))
+
+    def next_rows(layer, rows):
+        new = ((hid[rows, :].astype(jnp.float32) + branch[rows, :]) + bias_down[layer:layer + 1, :]).astype(jnp.bfloat16)
+        hid[rows, :] = new
+        return new.astype(jnp.float32)
+
+    def activate(step):
+        layer, slot = step // num_tiles, step % 2
+
+        @pl.loop(0, 2)
+        def _(which):
+            rows = pl.ds(pl.multiple_of(which * token_half, 128), token_half)
+
+            def slope(part):
+                cols = slice(part * UP_COLS, (part + 1) * UP_COLS)
+                act_buf[slot, rows, cols] = gelu(pre_buf[slot, rows, cols].astype(jnp.float32)).astype(jnp.bfloat16)
+
+            parts = tile_cols // UP_COLS
+            for part in range(parts):
+                cols = slice(part * UP_COLS, (part + 1) * UP_COLS)
+                start = pl.multiple_of((step % num_tiles) * tile_cols + part * UP_COLS, 128)
+                bias = bias_up[pl.ds(layer, 1), pl.ds(start, UP_COLS)]
+                pre_buf[slot, rows, cols] = (
+                    jnp.dot(normed[rows, :], up_buf[slot, :, cols], preferred_element_type=jnp.float32) + bias
+                ).astype(jnp.bfloat16)
+                if part > 0:
+                    slope(part - 1)
+            slope(parts - 1)
+
+    def add_branch(step):
+        slot = step % 2
+
+        @pl.loop(0, row_dim // UP_COLS)
+        def _(part):
+            cols = pl.ds(pl.multiple_of(part * UP_COLS, 128), UP_COLS)
+            branch[:, cols] += jnp.dot(act_buf[slot], down_buf[slot, :, cols], preferred_element_type=jnp.float32)
+
+    each_block(first_rows)
+    normed_store = pltpu.make_async_copy(normed, normed_out.at[0], io_sem.at[1])
+    normed_store.start()
     branch[...] = jnp.zeros_like(branch)
 
-    @pl.loop(0, num_layers * steps)
-    def _(step):
-        layer, tile = step // steps, step % steps
-
-        @pl.when(tile < num_tiles)
-        def _():
+    for layer in range(num_layers):
+        @pl.loop(layer * num_tiles, (layer + 1) * num_tiles)
+        def _(step):
             up_load(step).wait()
 
-            @pl.when(tile + 1 < num_tiles)
+            @pl.when(step + 1 < num_steps)
             def _():
                 up_load(step + 1).start()
 
-        @pl.when(tile > 0)
-        def _():
-            down_load(step - 1).wait()
-
-            @pl.when(tile < num_tiles)
+            @pl.when(step > 1)
             def _():
-                down_load(step).start()
-
-        @pl.when((tile == num_tiles) & (layer + 1 < num_layers))
-        def _():
-            up_load(step + 1).start()
-            down_load(step + 1).start()
-
-        @pl.when((tile > 1) & (tile < num_tiles))
-        def _():
-            for copy in tile_stores(step - 2):
-                copy.wait()
-
-        @pl.when(tile == 0)
-        def _():
-            @pl.when(layer > 0)
-            def _():
-                normed_store(layer - 1).wait()
-            norm_rows(layer)
-            normed_store(layer).start()
-            work(step, True, False)
-
-        @pl.when((tile > 0) & (tile < num_tiles))
-        def _():
-            work(step, True, True)
-
-        @pl.when(tile < num_tiles)
-        def _():
+                for copy in tile_stores(step - 2):
+                    copy.wait()
+            activate(step)
             for copy in tile_stores(step):
                 copy.start()
-
-        @pl.when(tile == num_tiles)
-        def _():
-            work(step, False, True)
-            for back in (2, 1):
-                for copy in tile_stores(step - back):
-                    copy.wait()
-            add_branch(layer)
-
-            @pl.when(layer + 1 < num_layers)
+            down_load(step).wait()
+
+            @pl.when(step + 1 < num_steps)
             def _():
-                hid_store().start()
-                branch[...] = jnp.zeros_like(branch)
-                hid_store().wait()
-
-    normed_store(num_layers - 1).wait()
+                down_load(step + 1).start()
+            add_branch(step)
+
+        normed_store.wait()
+        if layer + 1 < num_layers:
+            def to_next(rows, layer=layer):
+                normalize(layer + 1, rows, next_rows(layer, rows))
+                branch[rows, :] = jnp.zeros((NORM_ROWS, row_dim), jnp.float32)
+            each_block(to_next)
+            hid_store = pltpu.make_async_copy(hid, hid_out, io_sem.at[2])
+            hid_store.start()
+            normed_store = pltpu.make_async_copy(normed, normed_out.at[layer + 1], io_sem.at[1])
+            normed_store.start()
+
+    hid_store.wait()
     upstream_load.wait()
-    small_out[...] = jnp.zeros_like(small_out)
     bias_start = small_out.shape[1] - row_dim
 
-    @pl.loop(0, num_tokens // NORM_ROWS)
-    def _(block):
-        rows = pl.ds(pl.multiple_of(block * NORM_ROWS, NORM_ROWS), NORM_ROWS)
-        top_f = hid[rows, :].astype(jnp.float32)
+    def top_rows(rows):
+        top_f = next_rows(num_layers - 1, rows)
         top_scale = inverse_rms(top_f)
         top_hat = top_f * top_scale
         up_f = up_rows[rows, :].astype(jnp.float32)
@@ -196,10 +173,15 @@
         branch[rows, :] = grad
         grad_b_buf[rows, :] = grad.astype(jnp.bfloat16)
         small_out[:, bias_start:bias_start + row_dim] += jnp.sum(grad, axis=0, keepdims=True)
+
+    each_block(top_rows)
     grad_store = pltpu.make_async_copy(branch, grad_top_out, io_sem.at[0])
     grad_b_store = pltpu.make_async_copy(grad_b_buf, grad_top_b_out, io_sem.at[1])
     grad_store.start()
     grad_b_store.start()
+    for back in (2, 1):
+        for copy in tile_stores(jnp.int32(num_steps - back)):
+            copy.wait()
     grad_store.wait()
     grad_b_store.wait()
 
@@ -688,7 +670,7 @@
         hidden_width = w_up.shape[2]
         chunk_cols = width // 2
         hid_1, normed, pre_act, activated, grad_top, grad_top_b, small = forward_pass(
-            tokens, upstream, norm_gain, w_up, bias_up, w_down, bias_down, chunk_cols)
+            tokens, upstream, norm_gain, w_up, bias_up, w_down, bias_down, width)
         gathered, small = backward_pass(
             (tokens, hid_1), (normed, pre_act, activated), grad_top, grad_top_b, norm_gain, w_up, w_down, small, axis, chunk_cols)
         up_full, down_full = widen(gathered, num_layers, width, hidden_width, chunk_cols)

time: 796 us -> 708 us (0.89)
  Pallas kernels: 787 us -> 698 us
    pallas_call x1, Pallas kernels: 198 us -> 110 us  [forward_pass(): pl.pallas_call(functools.partial(forward_kernel, (num_layers, hidden // t...]
where the time goes in v5:
time: 708 us; the launch traced here: 706 us
  Pallas kernels  698 us (99%)
    pallas_call x1, Pallas kernels, backward_pass(): pl.pallas_call(functools.partial(backward_kernel, sizes), out_shape=(jax....  509 us
    pallas_call x1, Pallas kernels, forward_pass(): pl.pallas_call(functools.partial(forward_kernel, (num_layers, hidden // t...  110 us
    pallas_call x2, Pallas kernels, widen(): pl.pallas_call(widen_kernel, grid=(num_layers, per_mat), in_specs=[pl.Blo...  79.3 us

profile of v5, /device:TPU:0, one launch (start us, length us, event | category | flops | bytes accessed | tf_op | source)
XLA Modules:
  0.0 706.5 jit_solution(15755935595736848429)
XLA Ops:
  0.6 1.3 convert_element_type.10.gain_in.refs_9_
  1.9 1.3 convert_element_type.12.bias_down
  3.2 1.4 convert_element_type.11.bias_up
  4.6 109.9 %forward.1 = (bf16[1024,1536]{1,0:T(8,128)(2,1)}, bf16[2,1024,1536]{2,1,0:T(8,128)(2,1)}, bf16[2,1024,6144]{2,1,0:T(8,128)(2,1)}, bf16[2,1024,6144]{2,1,0:T(8,12...) custom-call(bf16[1024,1536]{1,0:T(8,128)(2,1)} %refs_0_.1, ...), custom_call_target="tpu_custom_call" | custom-call | tf_op jit(solution)/shard_map/forward/pallas_call | solution.py:198
  114.5 509.2 %backward.1 = (bf16[32,2,3,256,768]{4,3,2,1,0:T(8,128)(2,1)}, f32[1,18432]{1,0:T(1,128)}, bf16[8,1024,768]{2,1,0:T(8,128)(2,1)}, bf16[1024,1536]{1,0:T(8,128)(2,1)}) custom-call(bf16[1024,1536]{1,0:T(8,128)(2,1)} %refs_0_.1, bf16[1024,1536]{1,0:T(8,128)(2,1)} %get-tuple-element.14.refs_1_, bf16[2,1024,1536]{2,1,0:T(8,128)(2,1)} %get-tuple-element.15.refs_2_, ...), custom_call_target="tpu_custom_call" | custom-call | tf_op jit(solution)/shard_map/backward/pallas_call | solution.py:590
  623.6 0.5 broadcast.3
  624.2 1.7 reduce.3
  625.9 0.6 fusion
  626.5 0.6 slice.13
  627.1 39.7 %widen_down.1 = f32[2,6144,1536]{2,1,0:T(8,128)} custom-call(bf16[32,1536,768]{2,1,0:T(8,128)(2,1)} %bitcast.chunk_ref), custom_call_target="tpu_custom_call" | custom-call | tf_op jit(solution)/shard_map/widen_down/pallas_call | solution.py:654
  666.8 39.7 %widen_up.1 = f32[2,1536,6144]{2,1,0:T(8,128)} custom-call(bf16[32,1536,768]{2,1,0:T(8,128)(2,1)} %bitcast.chunk_ref), custom_call_target="tpu_custom_call" | custom-call | tf_op jit(solution)/shard_map/widen_up/pallas_call | solution.py:646
  (1 shorter events, 0.0 us)
